TPU v7x, 32 devices: a whole 2x2x4 slice. The times are simulated.
32 devices in a mesh: groups: 2 (over x), samp: 16 (over z, y, core).
Axes of the slice: x: 2, y: 2, z: 4, core: 2. Of those that a mesh axis runs over, the one named last changes fastest.
Arguments:
- dosage: bfloat16 [8192, 8192], P(('groups', 'samp')), parts along dimension 0, may hold values from 0 to 2
- covariates: bfloat16 [8192, 96], P(('groups', 'samp')), parts along dimension 0, may hold values from -8 to 8
- expression: bfloat16 [8192, 8192], P('groups', 'samp'), parts along dimension 0, may hold values from -10 to 10
- block_index: int32 [4, 1024], P('groups'), parts along dimension 0, may hold values from 0 to 8191
- expr_row: int32 [8192], P('groups'), parts along dimension 0, may hold values from 0 to 4095, each once
Outputs:
- zscore: float32 [4096, 8192], P('groups', 'samp'), parts along dimension 0
There are 2 independent parts, one for each index of `groups`. A program takes and returns all parts, laid end to end along the dimension named above; each array names one. Nothing has to cross between parts.
Inputs may be any that keep to these rules, and one draw needn't show every extreme that they name: `expr_row`: every expression row appears once.
All inputs are finite; a program needn't handle non-finite values.
Results may differ from a plain program's by a relative error of at most 0.0029.
Values may be sent and summed in bfloat16 or wider, within the bound.
No kernel may reach another device: no remote copies, remote signals or barrier semaphores. Data moves between devices by JAX's collectives and lax.ppermute only.
A program may use at most 192 MiB of HBM per device.

v0:
```python
import functools
import math

import jax
import jax.numpy as jnp
from jax import lax
from jax.experimental import pallas as pl
from jax.experimental.pallas import tpu as pltpu
from jax.sharding import PartitionSpec as P


epsilon = 1e-06
LANES = 128
PARTS = 2


def dot32(a, b):
    return jnp.dot(a, b, preferred_element_type=jnp.float32)


def gather_rows(dst, src, idx_ref, base, rows, nl, unroll=32):
    def body(j, _):
        first = pl.multiple_of(j * unroll, unroll)
        for u in range(unroll):
            i = idx_ref[base + first + u]
            dst[pl.ds(pl.multiple_of((first + u) * nl, nl), nl), :] = src[
                pl.ds(pl.multiple_of(i * nl, nl), nl), :
            ]
        return 0

    lax.fori_loop(0, rows // unroll, body, 0)


def limit(mib):
    return pltpu.CompilerParams(vmem_limit_bytes=mib * 2**20)


def held(array):
    return pltpu.with_memory_space_constraint(array, pltpu.VMEM)


HELD = pl.BlockSpec(memory_space=pltpu.VMEM)


def pick_kernel(idx_ref, x_hbm, o_ref, x_ref, t_ref, g_ref, sems):
    rows, n = x_ref.shape
    nl = rows // LANES
    width = o_ref.shape[0]
    step = 1024
    copies = [
        pltpu.make_async_copy(x_hbm.at[:, pl.ds(k, step)], x_ref.at[:, pl.ds(k, step)], sems.at[j])
        for j, k in enumerate(range(0, n, step))
    ]
    for copy in copies:
        copy.start()
    for copy, k in zip(copies, range(0, n, step)):
        copy.wait()
        v = x_ref[:, k : k + step].astype(jnp.float32).T
        for l in range(nl):
            t_ref[pl.ds(k * nl + l, step, stride=nl), :] = v[:, l * LANES : (l + 1) * LANES]
    gather_rows(g_ref, t_ref, idx_ref, 0, width, nl)
    for l in range(nl):
        o_ref[:, l * LANES : (l + 1) * LANES] = g_ref[pl.ds(l, width, stride=nl), :].astype(
            jnp.bfloat16
        )


def pick(x, idx):
    rows, n = x.shape
    (width,) = idx.shape
    nl = rows // LANES
    return pl.pallas_call(
        pick_kernel,
        grid_spec=pltpu.PrefetchScalarGridSpec(
            num_scalar_prefetch=1,
            grid=(1,),
            in_specs=[pl.BlockSpec(memory_space=pltpu.HBM)],
            out_specs=pl.BlockSpec((width, rows), lambda b, i: (0, 0)),
            scratch_shapes=[
                pltpu.VMEM((rows, n), jnp.bfloat16),
                pltpu.VMEM((n * nl, LANES), jnp.float32),
                pltpu.VMEM((width * nl, LANES), jnp.float32),
                pltpu.SemaphoreType.DMA((n // 1024,)),
            ],
        ),
        out_shape=jax.ShapeDtypeStruct((width, rows), jnp.bfloat16),
        compiler_params=limit(20),
        name="pick",
    )(idx, x)


def match_kernel(idx_ref, table_ref, me_ref, e_hbm, o_ref, norm_ref, e_ref, f_ref, g_ref, sems, *, chips):
    n, genes = e_ref.shape
    nl = genes // LANES
    rows = n // (2 * chips)
    step = 512
    copies = [
        pltpu.make_async_copy(e_hbm.at[pl.ds(k, step), :], e_ref.at[pl.ds(k, step), :], sems.at[j])
        for j, k in enumerate(range(0, n, step))
    ]
    for copy in copies:
        copy.start()
    total = jnp.zeros((8, genes), jnp.float32)
    for copy, k in zip(copies, range(0, n, step)):
        copy.wait()
        v = e_ref[k : k + step, :].astype(jnp.float32)
        for l in range(nl):
            f_ref[pl.ds(k * nl + l, step, stride=nl), :] = v[:, l * LANES : (l + 1) * LANES]
        total = total + jnp.sum((v * v).reshape(step // 8, 8, genes), axis=0)
    norm_ref[...] = jnp.sum(total, axis=0, keepdims=True)

    me = me_ref[0]
    spot = table_ref[me // 2]

    def shard(k, _):
        far = k // chips
        place = lax.rem(spot - table_ref[2 * chips + k - far * chips] + 2 * chips, chips)
        core = lax.rem(me + far, 2)
        first = (2 * table_ref[chips + place] + core) * rows
        gather_rows(g_ref, f_ref, idx_ref, first, rows, nl)
        here = pl.ds(pl.multiple_of(k * rows, rows), rows)
        for l in range(nl):
            o_ref[here, l * LANES : (l + 1) * LANES] = g_ref[pl.ds(l, rows, stride=nl), :].astype(
                jnp.bfloat16
            )
        return 0

    lax.fori_loop(0, 2 * chips, shard, 0)


def match(e, idx, table, me, chips):
    n, genes = e.shape
    nl = genes // LANES
    rows = n // (2 * chips)
    return pl.pallas_call(
        functools.partial(match_kernel, chips=chips),
        grid_spec=pltpu.PrefetchScalarGridSpec(
            num_scalar_prefetch=3,
            grid=(1,),
            in_specs=[pl.BlockSpec(memory_space=pltpu.HBM)],
            out_specs=[HELD, pl.BlockSpec((1, genes), lambda b, *_: (0, 0))],
            scratch_shapes=[
                pltpu.VMEM((n, genes), jnp.bfloat16),
                pltpu.VMEM((n * nl, LANES), jnp.float32),
                pltpu.VMEM((rows * nl, LANES), jnp.float32),
                pltpu.SemaphoreType.DMA((n // 512,)),
            ],
        ),
        out_shape=[
            pltpu.VMEM((n, genes), jnp.bfloat16),
            jax.ShapeDtypeStruct((1, genes), jnp.float32),
        ],
        compiler_params=limit(16 * n // 4096 + 2),
        name="match",
    )(idx, table, me, e)


def fold_sums(xs, e_ref, mine, theirs, at, sums):
    p, l, q = sums
    half = len(xs) // 2
    n = e_ref.shape[0]
    for far, c in enumerate((mine, theirs)):
        parts = [r[...] for r in xs[far * half : (far + 1) * half]]
        x = parts[0] if half == 1 else jnp.concatenate(parts, axis=1)
        depth = x.shape[1]
        first = far * (n // 2) + at * (depth // half)
        p = p + dot32(x, e_ref[first : first + depth, :])
        l = l + lax.dot_general(
            x, c, (((1,), (1,)), ((), ())), preferred_element_type=jnp.float32
        )
        f = x.astype(jnp.float32)
        f = f * f
        for j in range(depth // LANES):
            q = q + f[:, j * LANES : (j + 1) * LANES]
    return p, l, q


def fold_kernel(*refs, pieces, at, fresh, tile):
    xs = refs[:pieces]
    e_ref, mine_ref, theirs_ref = refs[pieces : pieces + 3]
    outs = refs[-3:]
    here = pl.ds(pl.multiple_of(pl.program_id(0) * tile, tile), tile)
    if fresh:
        sums = tuple(jnp.zeros((tile, o.shape[1]), jnp.float32) for o in outs)
    else:
        sums = tuple(r[here, :] for r in refs[pieces + 3 : pieces + 6])
    for o, v in zip(outs, fold_sums(xs, e_ref, mine_ref[...], theirs_ref[...], at, sums)):
        o[here, :] = v


def fold(xs, e, cov, at, sums, tile=256):
    pieces = len(xs)
    width, s = xs[0].shape
    genes = e.shape[1]
    covars = cov[0].shape[0]
    depth = pieces // 2 * s
    blk = at * s // depth
    assert blk * depth == at * s
    widths = (genes, covars, LANES)
    in_specs = [pl.BlockSpec((tile, s), lambda i: (i, 0))] * pieces + [HELD]
    in_specs += [pl.BlockSpec((covars, depth), lambda i: (0, blk))] * 2
    args = list(xs) + [held(e), *cov]
    aliases = {}
    if sums is not None:
        aliases = {pieces + 3 + k: k for k in range(3)}
        in_specs += [HELD] * 3
        args += [held(a) for a in sums]
    return pl.pallas_call(
        functools.partial(fold_kernel, pieces=pieces, at=at, fresh=sums is None, tile=tile),
        grid=(width // tile,),
        in_specs=in_specs,
        out_specs=[HELD] * 3,
        out_shape=[pltpu.VMEM((width, w), jnp.float32) for w in widths],
        input_output_aliases=aliases,
        compiler_params=limit(20),
        name="fold",
    )(*args)


def thirds(a):
    high = a.astype(jnp.bfloat16)
    rest = a - high.astype(jnp.float32)
    mid = rest.astype(jnp.bfloat16)
    low = (rest - mid.astype(jnp.float32)).astype(jnp.bfloat16)
    return high, mid, low


def solve_kernel(mine_ref, theirs_ref, e_ref, o_ref):
    size = mine_ref.shape[0]
    n, genes = e_ref.shape
    pitch = o_ref.shape[0] // 6
    across = (((1,), (1,)), ((), ()))
    mine, theirs = mine_ref[...], theirs_ref[...]
    m = lax.dot_general(mine, mine, across, preferred_element_type=jnp.float32)
    m = m + lax.dot_general(theirs, theirs, across, preferred_element_type=jnp.float32)
    cross = dot32(mine, e_ref[: n // 2, :]) + dot32(theirs, e_ref[n // 2 :, :])
    line = lax.broadcasted_iota(jnp.int32, (size, size), 0)
    lane = lax.broadcasted_iota(jnp.int32, (size, size), 1)
    for k in range(size):
        below = line[:, :1] > k
        factor = jnp.where(below, m[:, k : k + 1] / m[k : k + 1, k : k + 1], 0.0)
        row = jnp.where(lane[:1] == k, 1.0, m[k : k + 1, :])
        m = jnp.where((lane == k) & (line > k), 0.0, m) - factor * row
    pivot = jnp.sum(jnp.where(lane == line, m, 0.0), axis=1, keepdims=True)
    inverse = jnp.where(lane < line, m, jnp.where(lane == line, 1.0, 0.0)) * lax.rsqrt(pivot)
    high = functools.partial(
        lax.dot_general, precision=lax.Precision.HIGHEST, preferred_element_type=jnp.float32
    )
    down = (((0,), (0,)), ((), ()))
    slope = high(inverse, high(inverse, cross, (((1,), (0,)), ((), ()))), down)
    o_ref[...] = jnp.zeros(o_ref.shape, jnp.bfloat16)
    for first, part in ((0, slope), (genes, inverse.T)):
        h, i, l = thirds(part)
        for k, term in enumerate((h, i, l, h, i, h)):
            o_ref[k * pitch : k * pitch + size, first : first + part.shape[1]] = term


def solve(cov, e):
    size = cov[0].shape[0]
    pitch = size + -size % LANES
    _, genes = e.shape
    whole = lambda a: pl.BlockSpec(a.shape, lambda i: (0, 0))
    table = jax.ShapeDtypeStruct((6 * pitch, genes + pitch), jnp.bfloat16)
    return pl.pallas_call(
        solve_kernel,
        grid=(1,),
        in_specs=[whole(cov[0]), whole(cov[1]), HELD],
        out_specs=whole(table),
        out_shape=table,
        compiler_params=limit(20),
        name="solve",
    )(*cov, held(e))


def finish_kernel(*refs, pieces, at, scale, start):
    xs = refs[:pieces]
    e_ref, mine_ref, theirs_ref, p_ref, l_ref, q_ref, d_ref, norm_ref = refs[pieces : pieces + 8]
    o_ref = refs[-1]
    tile, genes = o_ref.shape
    here = pl.ds(pl.multiple_of(start + pl.program_id(0) * tile, tile), tile)
    sums = tuple(r[here, :] for r in (p_ref, l_ref, q_ref))
    p, l, q = fold_sums(xs, e_ref, mine_ref[...], theirs_ref[...], at, sums)
    blank = -l.shape[1] % LANES
    if blank:
        l = jnp.concatenate([l, jnp.zeros((tile, blank), jnp.float32)], axis=1)
    h, i, o = thirds(l)
    t = dot32(jnp.concatenate([h, h, h, i, i, o], axis=1), d_ref[...])
    w = t[:, genes:]
    resid_norm = jnp.sum(q, axis=1, keepdims=True) - jnp.sum(w * w, axis=1, keepdims=True)
    resid_norm = jnp.maximum(resid_norm, 0.0)
    o_ref[...] = (
        (p - t[:, :genes])
        * (scale * lax.rsqrt(resid_norm + epsilon))
        * lax.rsqrt(norm_ref[...] + epsilon)
    )


def finish(xs, e, cov, at, sums, d, norm, scale, start, block, blocks, out, tile=256):
    pieces = len(xs)
    width = sums[0].shape[0]
    rows, s = xs[0].shape
    genes = e.shape[1]
    covars = cov[0].shape[0]
    depth = pieces // 2 * s
    blk = at * s // depth
    assert blk * depth == at * s
    whole = lambda a: pl.BlockSpec(a.shape, lambda i: (0, 0))
    in_specs = [pl.BlockSpec((tile, s), lambda i: (i, 0))] * pieces + [HELD]
    in_specs += [pl.BlockSpec((covars, depth), lambda i: (0, blk))] * 2
    in_specs += [HELD] * 3 + [whole(d), whole(norm)]
    args = list(xs) + [held(e), *cov, *(held(a) for a in sums), d, norm]
    aliases = {}
    if out is not None:
        in_specs.append(pl.BlockSpec(memory_space=pl.ANY))
        aliases = {len(args): 0}
        args.append(out)
    first = (block * width + start) // tile
    return pl.pallas_call(
        functools.partial(finish_kernel, pieces=pieces, at=at, scale=scale, start=start),
        grid=(rows // tile,),
        in_specs=in_specs,
        out_specs=pl.BlockSpec((tile, genes), lambda i: (first + i, 0)),
        out_shape=jax.ShapeDtypeStruct((blocks * width, genes), jnp.float32),
        input_output_aliases=aliases,
        compiler_params=limit(20),
        name="finish",
    )(*args)


def ring_of(mesh):
    line = mesh.devices.reshape(mesh.shape["groups"], mesh.shape["samp"])[0]
    chips = line.shape[0] // 2
    plain = list(range(chips))
    spots = [tuple(getattr(line[2 * k], "coords", (0, 0, k))) for k in plain]
    wide = [a for a in range(3) if len({s[a] for s in spots}) > 1]
    if len(wide) == 2:
        short, long = sorted(wide, key=lambda a: len({s[a] for s in spots}))
        sides = sorted({s[short] for s in spots})
        if len(sides) == 2:
            up = sorted((k for k in plain if spots[k][short] == sides[0]), key=lambda k: spots[k][long])
            down = sorted((k for k in plain if spots[k][short] == sides[1]), key=lambda k: -spots[k][long])
            return up + down
    return plain


def local(ring, dosage, covariates, expression, block_index, expr_row):
    blocks = block_index.shape[0]
    samples = expr_row.shape[0]
    here, covars = covariates.shape
    scale = math.sqrt(samples - covars - 1)
    chips = len(ring)
    half = chips // 2

    def shift(x, by):
        pairs = [
            (2 * ring[k] + core, 2 * ring[(k + by) % chips] + core)
            for k in range(chips)
            for core in range(2)
        ]
        return lax.ppermute(x, "samp", pairs)

    def swap(x):
        return lax.ppermute(x, "samp", [(k, k ^ 1) for k in range(2 * chips)])

    order = []
    for d in range(1, half):
        order += [d, -d]
    order += [0, half]

    known = {0: covariates.T}
    for d in range(1, half + 1):
        known[d] = shift(known[d - 1], 1)
        if d < half:
            known[-d] = shift(known[1 - d], -1)
    mine = jnp.concatenate([known[o] for o in order], axis=1)
    cov = (mine, swap(mine))

    place = [0] * chips
    for k, chip in enumerate(ring):
        place[chip] = k
    table = jnp.array(place + ring + order, jnp.int32)
    me = lax.axis_index("samp").reshape(1)

    dosage = pltpu.with_memory_space_constraint(dosage, pltpu.HBM)
    expression = pltpu.with_memory_space_constraint(expression, pltpu.HBM)
    picks = []
    for b in range(blocks):
        picks.append(pick(dosage, block_index[b]))
    matched, panel_norm = match(expression, expr_row, table, me, chips)
    back = solve(cov, matched)

    sums = []
    for b in range(blocks):
        other = swap(picks[b])
        sums.append(fold([picks[b], other], matched, cov, 2 * half - 2, None))
    right = list(picks)
    left = list(picks)
    for d in range(1, half):
        for b in range(blocks):
            right[b] = shift(right[b], 1)
            left[b] = shift(left[b], -1)
            near = swap(right[b])
            far = swap(left[b])
            pieces = [right[b], left[b], near, far]
            sums[b] = fold(pieces, matched, cov, 2 * d - 2, sums[b])
    width = picks[0].shape[0]
    rows = width // PARTS
    out = None
    for part in range(PARTS):
        for b in range(blocks):
            here = slice(part * rows, (part + 1) * rows)
            last = shift(right[b][here], 1) if b % 2 == 0 else shift(left[b][here], -1)
            other = swap(last)
            out = finish(
                [last, other], matched, cov, 2 * half - 1, sums[b], back, panel_norm,
                scale, part * rows, b, blocks, out,
            )
    return out


def solution(mesh):
    placed = (
        P(("groups", "samp"), None),
        P(("groups", "samp"), None),
        P("groups", "samp"),
        P("groups", None),
        P("groups"),
    )
    ring = ring_of(mesh)

    def body(*args):
        return local(ring, *args)

    return jax.shard_map(
        body, mesh=mesh, in_specs=placed, out_specs=P("groups", "samp"), check_vma=False
    )
```

profile of v0, /device:TPU:0, one launch (start us, length us, event | category | flops | bytes accessed | tf_op | source)
XLA Modules:
  0.0 172.7 jit_solution(15782344239271470255)
XLA Ops:
  0.0 3.1 %collective-permute-start.5 = (bf16[96,256]{1,0:T(8,128)(2,1)}, bf16[96,256]{1,0:T(8,128)(2,1)S(1)}, u32[]{:S(2)}, u32[]{:S(2)}) collective-permute-start(bf16[96,256]{1,0:T(8,128)(2,1)} %bitcast.7), channel_id=1, source_target_pairs={{0,4},{1,5},{4,8},{5,9},{8,12},{9,13},{12,14},{13,15},{14,10},{15,... | collective-permute-start | bytes 147464 | tf_op jit(solution)/shard_map/ppermute | solution.py:360
  3.8 4.6 %pick.3.refs_0_ = bf16[1024,256]{1,0:T(8,128)(2,1)S(1)} custom-call(s32[1024]{0:T(1024)S(1)} %bitcast.6, bf16[256,8192]{1,0:T(8,128)(2,1)} %x_hbm.3), custom_call_target="tpu_custom_call" | custom-call | tf_op jit(solution)/shard_map/pick/pallas_call | solution.py:72
  10.7 4.6 %pick.2.refs_0_ = bf16[1024,256]{1,0:T(8,128)(2,1)S(1)} custom-call(s32[1024]{0:T(1024)S(1)} %bitcast.5, bf16[256,8192]{1,0:T(8,128)(2,1)} %x_hbm.3), custom_call_target="tpu_custom_call" | custom-call | tf_op jit(solution)/shard_map/pick/pallas_call | solution.py:72
  17.5 6.7 %collective-permute-done.7 = bf16[96,256]{1,0:T(8,128)(2,1)S(1)} collective-permute-done((bf16[96,256]{1,0:T(8,128)(2,1)S(1)}, bf16[96,256]{1,0:T(8,128)(2,1)S(1)}, u32[]{:S(2)}, u32[]{:S(2)}) %collective-permute-start.7) | collective-permute-done | bytes 49184 | tf_op jit(solution)/shard_map/ppermute | solution.py:360
  38.2 2.8 %collective-permute-done.11 = bf16[96,256]{1,0:T(8,128)(2,1)S(1)} collective-permute-done((bf16[96,256]{1,0:T(8,128)(2,1)S(1)}, bf16[96,256]{1,0:T(8,128)(2,1)S(1)}, u32[]{:S(2)}, u32[]{:S(2)}) %collective-permute-start.11) | collective-permute-done | bytes 49184 | tf_op jit(solution)/shard_map/ppermute | solution.py:360
  45.4 7.0 %collective-permute-done.13.refs_0_ = bf16[1024,256]{1,0:T(8,128)(2,1)S(1)} collective-permute-done((bf16[1024,256]{1,0:T(8,128)(2,1)S(1)}, bf16[1024,256]{1,0:T(8,128)(2,1)S(1)}, u32[]{:S(2)}, u32[]{:S(2)}) %collective-permute-start.13) | collective-permute-done | bytes 524320 | tf_op jit(solution)/shard_map/ppermute | solution.py:360
  64.1 4.3 %collective-permute-done.29.refs_1_ = bf16[1024,256]{1,0:T(8,128)(2,1)S(1)} collective-permute-done((bf16[1024,256]{1,0:T(8,128)(2,1)S(1)}, bf16[1024,256]{1,0:T(8,128)(2,1)S(1)}, u32[]{:S(2)}, u32[]{:S(2)}) %collective-permute-start.29) | collective-permute-done | bytes 524320 | tf_op jit(solution)/shard_map/ppermute | solution.py:360
  72.7 4.2 %collective-permute-done.1.refs_1_ = bf16[1024,256]{1,0:T(8,128)(2,1)S(1)} collective-permute-done((bf16[1024,256]{1,0:T(8,128)(2,1)S(1)}, bf16[1024,256]{1,0:T(8,128)(2,1)S(1)}, u32[]{:S(2)}, u32[]{:S(2)}) %collective-permute-start.1) | collective-permute-done | bytes 524320 | tf_op jit(solution)/shard_map/ppermute | solution.py:360
  81.9 4.4 %collective-permute-done.25.refs_0_ = bf16[1024,256]{1,0:T(8,128)(2,1)S(1)} collective-permute-done((bf16[1024,256]{1,0:T(8,128)(2,1)S(1)}, bf16[1024,256]{1,0:T(8,128)(2,1)S(1)}, u32[]{:S(2)}, u32[]{:S(2)}) %collective-permute-start.25) | collective-permute-done | bytes 524320 | tf_op jit(solution)/shard_map/ppermute | solution.py:360
  87.5 4.2 %collective-permute-done.2.refs_1_ = bf16[1024,256]{1,0:T(8,128)(2,1)S(1)} collective-permute-done((bf16[1024,256]{1,0:T(8,128)(2,1)S(1)}, bf16[1024,256]{1,0:T(8,128)(2,1)S(1)}, u32[]{:S(2)}, u32[]{:S(2)}) %collective-permute-start.2) | collective-permute-done | bytes 524320 | tf_op jit(solution)/shard_map/ppermute | solution.py:360
  93.1 7.0 %collective-permute-done.30.refs_1_ = bf16[1024,256]{1,0:T(8,128)(2,1)S(1)} collective-permute-done((bf16[1024,256]{1,0:T(8,128)(2,1)S(1)}, bf16[1024,256]{1,0:T(8,128)(2,1)S(1)}, u32[]{:S(2)}, u32[]{:S(2)}) %collective-permute-start.30) | collective-permute-done | bytes 524320 | tf_op jit(solution)/shard_map/ppermute | solution.py:360
  107.3 2.9 %collective-permute-done.26.refs_0_ = bf16[512,256]{1,0:T(8,128)(2,1)} collective-permute-done((bf16[512,256]{1,0:T(8,128)(2,1)S(1)}, bf16[512,256]{1,0:T(8,128)(2,1)}, u32[]{:S(2)}, u32[]{:S(2)}) %collective-permute-start.26) | collective-permute-done | bytes 262176 | tf_op jit(solution)/shard_map/ppermute | solution.py:360
  111.8 4.9 %collective-permute-done.3.refs_0_ = bf16[512,256]{1,0:T(8,128)(2,1)} collective-permute-done((bf16[512,256]{1,0:T(8,128)(2,1)S(1)}, bf16[512,256]{1,0:T(8,128)(2,1)}, u32[]{:S(2)}, u32[]{:S(2)}) %collective-permute-start.3) | collective-permute-done | bytes 262176 | tf_op jit(solution)/shard_map/ppermute | solution.py:360
  120.2 9.0 %match.1 = (bf16[4096,512]{1,0:T(8,128)(2,1)S(1)}, f32[1,512]{1,0:T(1,128)S(1)}) custom-call(s32[4096]{0:T(1024)S(1)} %copy-done.42, s32[24]{0:T(128)S(1)} %copy-done.43, s32[1]{0:T(128)} %bitcast.1.me_ref, bf16[4096,512]{1,0:T(8,128)(2,1)} %e_hbm.1), custom_call_target="tpu_custom_call" | custom-call | tf_op jit(solution)/shard_map/match/pallas_call | solution.py:135
  129.2 9.3 %solve.1.refs_8_ = bf16[768,640]{1,0:T(8,128)(2,1)S(1)} custom-call(bf16[96,2048]{1,0:T(8,128)(2,1)S(1)} %constant_dynamic-update-slice_fusion.refs_3_.refs_5_.mine_ref, bf16[96,2048]{1,0:T(8,128)(2,1)S(1)} %collective-permute-done.12.refs_4_.refs_6_.theirs_ref, bf16[4096,512]{1,0:T(8,128)(2,1)S(1)} %get-tuple-element.31.refs_2_.refs_4_.e_ref), custom_call_target="tpu_custom_call" | custom-call | tf_op jit(solution)/shard_map/solve/pallas_call | solution.py:264
  141.7 2.4 %fold.13 = (f32[1024,512]{1,0:T(8,128)S(1)}, f32[1024,96]{1,0:T(8,128)S(1)}, f32[1024,128]{1,0:T(8,128)S(1)}) custom-call(bf16[1024,256]{1,0:T(8,128)(2,1)S(1)} %collective-permute-done.23.refs_0_, bf16[1024,256]{1,0:T(8,128)(2,1)S(1)} %copy-done.1, bf16[1024,256]{1,0:T(8,128)(2,1)S(1)} %copy-done.11, ...), custom_call_target="tpu_custom_call", output_to_operand_aliasing={{0}: (7, {}), {1}: (8, {}), {2}: (9, {})} | custom-call | tf_op jit(solution)/shard_map/fold/pallas_call | solution.py:208
  144.2 2.4 %fold.9 = (f32[1024,512]{1,0:T(8,128)S(1)}, f32[1024,96]{1,0:T(8,128)S(1)}, f32[1024,128]{1,0:T(8,128)S(1)}) custom-call(bf16[1024,256]{1,0:T(8,128)(2,1)S(1)} %copy-done.7, bf16[1024,256]{1,0:T(8,128)(2,1)S(1)} %copy-done.9, bf16[1024,256]{1,0:T(8,128)(2,1)S(1)} %copy-done.23, ...), custom_call_target="tpu_custom_call", output_to_operand_aliasing={{0}: (7, {}), {1}: (8, {}), {2}: (9, {})} | custom-call | tf_op jit(solution)/shard_map/fold/pallas_call | solution.py:208
  146.7 2.4 %fold.14 = (f32[1024,512]{1,0:T(8,128)S(1)}, f32[1024,96]{1,0:T(8,128)S(1)}, f32[1024,128]{1,0:T(8,128)S(1)}) custom-call(bf16[1024,256]{1,0:T(8,128)(2,1)S(1)} %copy-done.13, bf16[1024,256]{1,0:T(8,128)(2,1)S(1)} %copy-done.15, bf16[1024,256]{1,0:T(8,128)(2,1)S(1)} %copy-done.27, ...), custom_call_target="tpu_custom_call", output_to_operand_aliasing={{0}: (7, {}), {1}: (8, {}), {2}: (9, {})} | custom-call | tf_op jit(solution)/shard_map/fold/pallas_call | solution.py:208
  149.2 2.4 %fold.10 = (f32[1024,512]{1,0:T(8,128)S(1)}, f32[1024,96]{1,0:T(8,128)S(1)}, f32[1024,128]{1,0:T(8,128)S(1)}) custom-call(bf16[1024,256]{1,0:T(8,128)(2,1)S(1)} %copy-done.21, bf16[1024,256]{1,0:T(8,128)(2,1)S(1)} %copy-done.19, bf16[1024,256]{1,0:T(8,128)(2,1)S(1)} %copy-done.33, ...), custom_call_target="tpu_custom_call", output_to_operand_aliasing={{0}: (7, {}), {1}: (8, {}), {2}: (9, {})} | custom-call | tf_op jit(solution)/shard_map/fold/pallas_call | solution.py:208
  154.1 3.8 %fold.11 = (f32[1024,512]{1,0:T(8,128)S(1)}, f32[1024,96]{1,0:T(8,128)S(1)}, f32[1024,128]{1,0:T(8,128)S(1)}) custom-call(bf16[1024,256]{1,0:T(8,128)(2,1)} %collective-permute-done.15.refs_0_, bf16[1024,256]{1,0:T(8,128)(2,1)S(1)} %collective-permute-done.2.refs_1_, ...), custom_call_target="tpu_custom_call", output_to_operand_aliasing={{0}: (7, {}), {1}: (8, {}), {2}: (9, {})} | custom-call | tf_op jit(solution)/shard_map/fold/pallas_call | solution.py:208
  157.9 3.7 %finish.4.refs_10_ = f32[2048,512]{1,0:T(8,128)} custom-call(bf16[512,256]{1,0:T(8,128)(2,1)} %collective-permute-done.40.refs_0_, bf16[512,256]{1,0:T(8,128)(2,1)} %collective-permute-done.41.refs_1_, bf16[4096,512]{1,0:T(8,128)(2,1)S(1)} %get-tuple-element.31.refs_2_.refs_4_.e_ref, ...), custom_call_target="tpu_custom_call" | custom-call | tf_op jit(solution)/shard_map/finish/pallas_call | solution.py:318
  161.6 3.7 %finish.5.refs_10_ = f32[2048,512]{1,0:T(8,128)} custom-call(bf16[512,256]{1,0:T(8,128)(2,1)} %collective-permute-done.38.refs_0_, bf16[512,256]{1,0:T(8,128)(2,1)} %collective-permute-done.39.refs_1_, bf16[4096,512]{1,0:T(8,128)(2,1)S(1)} %get-tuple-element.31.refs_2_.refs_4_.e_ref, ...), custom_call_target="tpu_custom_call", output_to_operand_aliasing={{}: (10, {})} | custom-call | tf_op jit(solution)/shard_map/finish/pallas_call | solution.py:318
  165.3 3.7 %finish.6.refs_10_ = f32[2048,512]{1,0:T(8,128)} custom-call(bf16[512,256]{1,0:T(8,128)(2,1)} %collective-permute-done.26.refs_0_, bf16[512,256]{1,0:T(8,128)(2,1)} %collective-permute-done.27.refs_1_, bf16[4096,512]{1,0:T(8,128)(2,1)S(1)} %get-tuple-element.31.refs_2_.refs_4_.e_ref, ...), custom_call_target="tpu_custom_call", output_to_operand_aliasing={{}: (10, {})} | custom-call | tf_op jit(solution)/shard_map/finish/pallas_call | solution.py:318
  169.0 3.7 %finish.7 = f32[2048,512]{1,0:T(8,128)} custom-call(bf16[512,256]{1,0:T(8,128)(2,1)} %collective-permute-done.3.refs_0_, bf16[512,256]{1,0:T(8,128)(2,1)} %collective-permute-done.4.refs_1_, bf16[4096,512]{1,0:T(8,128)(2,1)S(1)} %get-tuple-element.31.refs_2_.refs_4_.e_ref, ...), custom_call_target="tpu_custom_call", output_to_operand_aliasing={{}: (10, {})} | custom-call | tf_op jit(solution)/shard_map/finish/pallas_call | solution.py:318
  (177 shorter events, 65.0 us)
Async XLA Ops:
  0.0 15.3 %collective-permute-start.5 = (bf16[96,256]{1,0:T(8,128)(2,1)}, bf16[96,256]{1,0:T(8,128)(2,1)S(1)}, u32[]{:S(2)}, u32[]{:S(2)}) collective-permute-start(bf16[96,256]{1,0:T(8,128)(2,1)} %bitcast.7), channel_id=1, source_target_pairs={{0,4},{1,5},{4,8},{5,9},{8,12},{9,13},{12,14},{13,15},{14,10},{15,... | collective-permute-start | bytes 147464 | tf_op jit(solution)/shard_map/ppermute | solution.py:360
  8.5 34.4 %collective-permute-start.37 = (bf16[1024,256]{1,0:T(8,128)(2,1)S(1)}, bf16[1024,256]{1,0:T(8,128)(2,1)S(1)}, u32[]{:S(2)}, u32[]{:S(2)}) collective-permute-start(bf16[1024,256]{1,0:T(8,128)(2,1)S(1)} %pick.3.refs_0_), channel_id=1, source_target_pairs={{0,1},{1,0},{2,3},{3,2},{4,5},{5,4},{6,7},{7,6},{8,9},{9,8},{10,11... | collective-permute-start | bytes 1572872 | tf_op jit(solution)/shard_map/ppermute | solution.py:363
  8.6 35.4 %collective-permute-start.23 = (bf16[1024,256]{1,0:T(8,128)(2,1)S(1)}, bf16[1024,256]{1,0:T(8,128)(2,1)S(1)}, u32[]{:S(2)}, u32[]{:S(2)}) collective-permute-start(bf16[1024,256]{1,0:T(8,128)(2,1)S(1)} %pick.3.refs_0_), channel_id=1, source_target_pairs={{0,4},{1,5},{4,8},{5,9},{8,12},{9,13},{12,14},{13,15},{14,10},{15,... | collective-permute-start | bytes 1572872 | tf_op jit(solution)/shard_map/ppermute | solution.py:360
  10.6 33.3 %collective-permute-start.28 = (bf16[1024,256]{1,0:T(8,128)(2,1)S(1)}, bf16[1024,256]{1,0:T(8,128)(2,1)S(1)}, u32[]{:S(2)}, u32[]{:S(2)}) collective-permute-start(bf16[1024,256]{1,0:T(8,128)(2,1)S(1)} %pick.3.refs_0_), channel_id=1, source_target_pairs={{0,2},{1,3},{4,0},{5,1},{8,4},{9,5},{12,8},{13,9},{14,12},{15,13},... | collective-permute-start | bytes 1572872 | tf_op jit(solution)/shard_map/ppermute | solution.py:360
  15.3 29.2 %collective-permute-start.22 = (bf16[1024,256]{1,0:T(8,128)(2,1)S(1)}, bf16[1024,256]{1,0:T(8,128)(2,1)S(1)}, u32[]{:S(2)}, u32[]{:S(2)}) collective-permute-start(bf16[1024,256]{1,0:T(8,128)(2,1)S(1)} %pick.2.refs_0_), channel_id=1, source_target_pairs={{0,1},{1,0},{2,3},{3,2},{4,5},{5,4},{6,7},{7,6},{8,9},{9,8},{10,11... | collective-permute-start | bytes 1572872 | tf_op jit(solution)/shard_map/ppermute | solution.py:363
  43.9 12.9 %collective-permute-start.35 = (bf16[1024,256]{1,0:T(8,128)(2,1)S(1)}, bf16[1024,256]{1,0:T(8,128)(2,1)S(1)}, u32[]{:S(2)}, u32[]{:S(2)}) collective-permute-start(bf16[1024,256]{1,0:T(8,128)(2,1)S(1)} %collective-permute-done.23.refs_0_), channel_id=1, source_target_pairs={{0,1},{1,0},{2,3},{3,2},{4,5},{5,4},{6,7},{7,6},{8,9},{9,8},{10,11... | collective-permute-start | bytes 1572872 | tf_op jit(solution)/shard_map/ppermute | solution.py:363
  44.0 12.8 %collective-permute-start.12 = (bf16[96,2048]{1,0:T(8,128)(2,1)S(1)}, bf16[96,2048]{1,0:T(8,128)(2,1)S(1)}, u32[]{:S(2)}, u32[]{:S(2)}) collective-permute-start(bf16[96,2048]{1,0:T(8,128)(2,1)S(1)} %constant_dynamic-update-slice_fusion.refs_3_.refs_5_.mine_ref), channel_id=1, source_target_pairs={{0,1},{1,0},{2,3},{3,2},{4,5},{5,4},{6,7},{7,6},{8,9},{9,8},{10,11... | collective-permute-start | bytes 1179656 | tf_op jit(solution)/shard_map/ppermute | solution.py:363
  45.3 12.8 %collective-permute-start.36 = (bf16[1024,256]{1,0:T(8,128)(2,1)S(1)}, bf16[1024,256]{1,0:T(8,128)(2,1)S(1)}, u32[]{:S(2)}, u32[]{:S(2)}) collective-permute-start(bf16[1024,256]{1,0:T(8,128)(2,1)S(1)} %collective-permute-done.28.refs_1_), channel_id=1, source_target_pairs={{0,1},{1,0},{2,3},{3,2},{4,5},{5,4},{6,7},{7,6},{8,9},{9,8},{10,11... | collective-permute-start | bytes 1572872 | tf_op jit(solution)/shard_map/ppermute | solution.py:363
  58.9 17.9 %collective-permute-start.1 = (bf16[1024,256]{1,0:T(8,128)(2,1)S(1)}, bf16[1024,256]{1,0:T(8,128)(2,1)S(1)}, u32[]{:S(2)}, u32[]{:S(2)}) collective-permute-start(bf16[1024,256]{1,0:T(8,128)(2,1)S(1)} %collective-permute-done.refs_1_), channel_id=1, source_target_pairs={{0,2},{1,3},{4,0},{5,1},{8,4},{9,5},{12,8},{13,9},{14,12},{15,13},... | collective-permute-start | bytes 1572872 | tf_op jit(solution)/shard_map/ppermute | solution.py:360
  61.6 15.2 %collective-permute-start.14 = (bf16[1024,256]{1,0:T(8,128)(2,1)S(1)}, bf16[1024,256]{1,0:T(8,128)(2,1)S(1)}, u32[]{:S(2)}, u32[]{:S(2)}) collective-permute-start(bf16[1024,256]{1,0:T(8,128)(2,1)S(1)} %collective-permute-done.13.refs_0_), channel_id=1, source_target_pairs={{0,4},{1,5},{4,8},{5,9},{8,12},{9,13},{12,14},{13,15},{14,10},{15,... | collective-permute-start | bytes 1572872 | tf_op jit(solution)/shard_map/ppermute | solution.py:360
  70.5 15.9 %collective-permute-start.25 = (bf16[1024,256]{1,0:T(8,128)(2,1)S(1)}, bf16[1024,256]{1,0:T(8,128)(2,1)S(1)}, u32[]{:S(2)}, u32[]{:S(2)}) collective-permute-start(bf16[1024,256]{1,0:T(8,128)(2,1)S(1)} %collective-permute-done.24.refs_0_), channel_id=1, source_target_pairs={{0,4},{1,5},{4,8},{5,9},{8,12},{9,13},{12,14},{13,15},{14,10},{15,... | collective-permute-start | bytes 1572872 | tf_op jit(solution)/shard_map/ppermute | solution.py:360
  76.9 14.8 %collective-permute-start.2 = (bf16[1024,256]{1,0:T(8,128)(2,1)S(1)}, bf16[1024,256]{1,0:T(8,128)(2,1)S(1)}, u32[]{:S(2)}, u32[]{:S(2)}) collective-permute-start(bf16[1024,256]{1,0:T(8,128)(2,1)S(1)} %collective-permute-done.1.refs_1_), channel_id=1, source_target_pairs={{0,2},{1,3},{4,0},{5,1},{8,4},{9,5},{12,8},{13,9},{14,12},{15,13},... | collective-permute-start | bytes 1572872 | tf_op jit(solution)/shard_map/ppermute | solution.py:360
  76.9 23.2 %collective-permute-start.30 = (bf16[1024,256]{1,0:T(8,128)(2,1)S(1)}, bf16[1024,256]{1,0:T(8,128)(2,1)S(1)}, u32[]{:S(2)}, u32[]{:S(2)}) collective-permute-start(bf16[1024,256]{1,0:T(8,128)(2,1)S(1)} %collective-permute-done.29.refs_1_), channel_id=1, source_target_pairs={{0,2},{1,3},{4,0},{5,1},{8,4},{9,5},{12,8},{13,9},{14,12},{15,13},... | collective-permute-start | bytes 1572872 | tf_op jit(solution)/shard_map/ppermute | solution.py:360
  79.8 20.3 %collective-permute-start.18 = (bf16[1024,256]{1,0:T(8,128)(2,1)S(1)}, bf16[1024,256]{1,0:T(8,128)(2,1)S(1)}, u32[]{:S(2)}, u32[]{:S(2)}) collective-permute-start(bf16[1024,256]{1,0:T(8,128)(2,1)S(1)} %collective-permute-done.14.refs_0_), channel_id=1, source_target_pairs={{0,1},{1,0},{2,3},{3,2},{4,5},{5,4},{6,7},{7,6},{8,9},{9,8},{10,11... | collective-permute-start | bytes 1572872 | tf_op jit(solution)/shard_map/ppermute | solution.py:363
  80.6 22.3 %collective-permute-start.19 = (bf16[1024,256]{1,0:T(8,128)(2,1)S(1)}, bf16[1024,256]{1,0:T(8,128)(2,1)S(1)}, u32[]{:S(2)}, u32[]{:S(2)}) collective-permute-start(bf16[1024,256]{1,0:T(8,128)(2,1)S(1)} %collective-permute-done.1.refs_1_), channel_id=1, source_target_pairs={{0,1},{1,0},{2,3},{3,2},{4,5},{5,4},{6,7},{7,6},{8,9},{9,8},{10,11... | collective-permute-start | bytes 1572872 | tf_op jit(solution)/shard_map/ppermute | solution.py:363
  86.3 17.4 %collective-permute-start.15 = (bf16[1024,256]{1,0:T(8,128)(2,1)S(1)}, bf16[1024,256]{1,0:T(8,128)(2,1)}, u32[]{:S(2)}, u32[]{:S(2)}) collective-permute-start(bf16[1024,256]{1,0:T(8,128)(2,1)S(1)} %collective-permute-done.14.refs_0_), channel_id=1, source_target_pairs={{0,4},{1,5},{4,8},{5,9},{8,12},{9,13},{12,14},{13,15},{14,10},{15,... | collective-permute-start | bytes 1572872 | tf_op jit(solution)/shard_map/ppermute | solution.py:360
  91.7 15.2 %collective-permute-start.40 = (bf16[512,256]{1,0:T(8,128)(2,1)S(1)}, bf16[512,256]{1,0:T(8,128)(2,1)}, u32[]{:S(2)}, u32[]{:S(2)}) collective-permute-start(bf16[512,256]{1,0:T(8,128)(2,1)S(1)} %get-tuple-element.57), channel_id=1, source_target_pairs={{0,4},{1,5},{4,8},{5,9},{8,12},{9,13},{12,14},{13,15},{14,10},{15,... | collective-permute-start | bytes 786440 | tf_op jit(solution)/shard_map/ppermute | solution.py:360
  103.7 13.0 %collective-permute-start.31 = (bf16[1024,256]{1,0:T(8,128)(2,1)S(1)}, bf16[1024,256]{1,0:T(8,128)(2,1)S(1)}, u32[]{:S(2)}, u32[]{:S(2)}) collective-permute-start(bf16[1024,256]{1,0:T(8,128)(2,1)S(1)} %collective-permute-done.25.refs_0_), channel_id=1, source_target_pairs={{0,1},{1,0},{2,3},{3,2},{4,5},{5,4},{6,7},{7,6},{8,9},{9,8},{10,11... | collective-permute-start | bytes 1572872 | tf_op jit(solution)/shard_map/ppermute | solution.py:363
  103.7 14.3 %collective-permute-start.32 = (bf16[1024,256]{1,0:T(8,128)(2,1)S(1)}, bf16[1024,256]{1,0:T(8,128)(2,1)S(1)}, u32[]{:S(2)}, u32[]{:S(2)}) collective-permute-start(bf16[1024,256]{1,0:T(8,128)(2,1)S(1)} %collective-permute-done.30.refs_1_), channel_id=1, source_target_pairs={{0,1},{1,0},{2,3},{3,2},{4,5},{5,4},{6,7},{7,6},{8,9},{9,8},{10,11... | collective-permute-start | bytes 1572872 | tf_op jit(solution)/shard_map/ppermute | solution.py:363
  106.8 47.3 %collective-permute-start.16 = (bf16[1024,256]{1,0:T(8,128)(2,1)}, bf16[1024,256]{1,0:T(8,128)(2,1)}, u32[]{:S(2)}, u32[]{:S(2)}) collective-permute-start(bf16[1024,256]{1,0:T(8,128)(2,1)} %collective-permute-done.15.refs_0_), channel_id=1, source_target_pairs={{0,1},{1,0},{2,3},{3,2},{4,5},{5,4},{6,7},{7,6},{8,9},{9,8},{10,11... | collective-permute-start | bytes 1572872 | tf_op jit(solution)/shard_map/ppermute | solution.py:363
  116.7 41.2 %collective-permute-start.41 = (bf16[512,256]{1,0:T(8,128)(2,1)}, bf16[512,256]{1,0:T(8,128)(2,1)}, u32[]{:S(2)}, u32[]{:S(2)}) collective-permute-start(bf16[512,256]{1,0:T(8,128)(2,1)} %collective-permute-done.40.refs_0_), channel_id=1, source_target_pairs={{0,1},{1,0},{2,3},{3,2},{4,5},{5,4},{6,7},{7,6},{8,9},{9,8},{10,11... | collective-permute-start | bytes 786440 | tf_op jit(solution)/shard_map/ppermute | solution.py:363
  117.5 44.1 %collective-permute-start.39 = (bf16[512,256]{1,0:T(8,128)(2,1)}, bf16[512,256]{1,0:T(8,128)(2,1)}, u32[]{:S(2)}, u32[]{:S(2)}) collective-permute-start(bf16[512,256]{1,0:T(8,128)(2,1)} %collective-permute-done.38.refs_0_), channel_id=1, source_target_pairs={{0,1},{1,0},{2,3},{3,2},{4,5},{5,4},{6,7},{7,6},{8,9},{9,8},{10,11... | collective-permute-start | bytes 786440 | tf_op jit(solution)/shard_map/ppermute | solution.py:363
  118.9 46.5 %collective-permute-start.27 = (bf16[512,256]{1,0:T(8,128)(2,1)}, bf16[512,256]{1,0:T(8,128)(2,1)}, u32[]{:S(2)}, u32[]{:S(2)}) collective-permute-start(bf16[512,256]{1,0:T(8,128)(2,1)} %collective-permute-done.26.refs_0_), channel_id=1, source_target_pairs={{0,1},{1,0},{2,3},{3,2},{4,5},{5,4},{6,7},{7,6},{8,9},{9,8},{10,11... | collective-permute-start | bytes 786440 | tf_op jit(solution)/shard_map/ppermute | solution.py:363
  119.7 49.3 %collective-permute-start.4 = (bf16[512,256]{1,0:T(8,128)(2,1)}, bf16[512,256]{1,0:T(8,128)(2,1)}, u32[]{:S(2)}, u32[]{:S(2)}) collective-permute-start(bf16[512,256]{1,0:T(8,128)(2,1)} %collective-permute-done.3.refs_0_), channel_id=1, source_target_pairs={{0,1},{1,0},{2,3},{3,2},{4,5},{5,4},{6,7},{7,6},{8,9},{9,8},{10,11... | collective-permute-start | bytes 786440 | tf_op jit(solution)/shard_map/ppermute | solution.py:363
  (63 other events, 477.7 us)
where the time goes:
time: 173 us
  Pallas kernels  61.3 us (35%)
  waiting for transfers between devices  59.1 us (34%)
  starting transfers between devices  33.8 us (20%)
  local copies, waits for them, and re-layouts  17.8 us (10%)
    ppermute x23, waiting for transfers between devices, shift(): return lax.ppermute(x, 'samp', pairs)  59.1 us
    ppermute x23, starting transfers between devices, shift(): return lax.ppermute(x, 'samp', pairs)  29.4 us
    pallas_call x8, Pallas kernels, fold(): pl.pallas_call(functools.partial(fold_kernel, pieces=pieces, at=at, fresh...  19 us
    unnamed x97, local copies, waits for them, and re-layouts  17 us
    pallas_call x4, Pallas kernels, finish(): pl.pallas_call(functools.partial(finish_kernel, pieces=pieces, at=at, sca...  14.7 us
    pallas_call x2, Pallas kernels, pick(): pl.pallas_call(pick_kernel, grid_spec=pltpu.PrefetchScalarGridSpec(num_sc...  9.28 us
    pallas_call x1, Pallas kernels, solve(): pl.pallas_call(solve_kernel, grid=(1,), in_specs=[whole(cov[0]), whole(co...  9.26 us
    pallas_call x1, Pallas kernels, match(): pl.pallas_call(functools.partial(match_kernel, chips=chips), grid_spec=pl...  9.03 us
  transfers between devices with their start and end apart: 42, of which 16 were waited for; matrix products, arithmetic and copies ran while one was open for 1% of the time, Pallas kernels for 33%

commit v1 on v0

--- a/solution.py
+++ b/solution.py
@@ -11,18 +11,18 @@
 
 epsilon = 1e-06
 LANES = 128
-PARTS = 2
+PARTS = 1
 
 
 def dot32(a, b):
     return jnp.dot(a, b, preferred_element_type=jnp.float32)
 
 
-def gather_rows(dst, src, idx_ref, base, rows, nl, unroll=32):
+def gather_rows(dst, src, entry, rows, nl, unroll=32):
     def body(j, _):
         first = pl.multiple_of(j * unroll, unroll)
         for u in range(unroll):
-            i = idx_ref[base + first + u]
+            i = entry(first, u)
             dst[pl.ds(pl.multiple_of((first + u) * nl, nl), nl), :] = src[
                 pl.ds(pl.multiple_of(i * nl, nl), nl), :
             ]
@@ -55,10 +55,10 @@
         copy.start()
     for copy, k in zip(copies, range(0, n, step)):
         copy.wait()
-        v = x_ref[:, k : k + step].astype(jnp.float32).T
+        v = x_ref[:, k : k + step].T.astype(jnp.float32)
         for l in range(nl):
             t_ref[pl.ds(k * nl + l, step, stride=nl), :] = v[:, l * LANES : (l + 1) * LANES]
-    gather_rows(g_ref, t_ref, idx_ref, 0, width, nl)
+    gather_rows(g_ref, t_ref, lambda k, u: idx_ref[k + u], width, nl)
     for l in range(nl):
         o_ref[:, l * LANES : (l + 1) * LANES] = g_ref[pl.ds(l, width, stride=nl), :].astype(
             jnp.bfloat16
@@ -117,7 +117,7 @@
         place = lax.rem(spot - table_ref[2 * chips + k - far * chips] + 2 * chips, chips)
         core = lax.rem(me + far, 2)
         first = (2 * table_ref[chips + place] + core) * rows
-        gather_rows(g_ref, f_ref, idx_ref, first, rows, nl)
+        gather_rows(g_ref, f_ref, lambda k, u: idx_ref[first + k + u], rows, nl)
         here = pl.ds(pl.multiple_of(k * rows, rows), rows)
         for l in range(nl):
             o_ref[here, l * LANES : (l + 1) * LANES] = g_ref[pl.ds(l, rows, stride=nl), :].astype(
@@ -155,24 +155,24 @@
     )(idx, table, me, e)
 
 
-def fold_sums(xs, e_ref, mine, theirs, at, sums):
-    p, l, q = sums
-    half = len(xs) // 2
+def both_halves(xs, e_ref, at):
+    near = len(xs) // 2
     n = e_ref.shape[0]
-    for far, c in enumerate((mine, theirs)):
-        parts = [r[...] for r in xs[far * half : (far + 1) * half]]
-        x = parts[0] if half == 1 else jnp.concatenate(parts, axis=1)
-        depth = x.shape[1]
-        first = far * (n // 2) + at * (depth // half)
-        p = p + dot32(x, e_ref[first : first + depth, :])
-        l = l + lax.dot_general(
-            x, c, (((1,), (1,)), ((), ())), preferred_element_type=jnp.float32
-        )
-        f = x.astype(jnp.float32)
-        f = f * f
-        for j in range(depth // LANES):
-            q = q + f[:, j * LANES : (j + 1) * LANES]
-    return p, l, q
+    x = jnp.concatenate([r[...] for r in xs], axis=1)
+    depth = x.shape[1] // 2
+    first = at * (depth // near)
+    rows = [e_ref[k + first : k + first + depth, :] for k in (0, n // 2)]
+    return x, jnp.concatenate(rows, axis=0)
+
+
+def loads_and_squares(x, mine, theirs, l, q):
+    c = jnp.concatenate([mine, theirs], axis=1)
+    l = l + lax.dot_general(x, c, (((1,), (1,)), ((), ())), preferred_element_type=jnp.float32)
+    f = x.astype(jnp.float32)
+    f = f * f
+    for j in range(x.shape[1] // LANES):
+        q = q + f[:, j * LANES : (j + 1) * LANES]
+    return l, q
 
 
 def fold_kernel(*refs, pieces, at, fresh, tile):
@@ -181,21 +181,24 @@
     outs = refs[-3:]
     here = pl.ds(pl.multiple_of(pl.program_id(0) * tile, tile), tile)
     if fresh:
-        sums = tuple(jnp.zeros((tile, o.shape[1]), jnp.float32) for o in outs)
+        p, l, q = (jnp.zeros((tile, o.shape[1]), jnp.float32) for o in outs)
     else:
-        sums = tuple(r[here, :] for r in refs[pieces + 3 : pieces + 6])
-    for o, v in zip(outs, fold_sums(xs, e_ref, mine_ref[...], theirs_ref[...], at, sums)):
-        o[here, :] = v
-
-
-def fold(xs, e, cov, at, sums, tile=256):
+        p, l, q = (r[here, :] for r in refs[pieces + 3 : pieces + 6])
+    x, e = both_halves(xs, e_ref, at)
+    outs[0][here, :] = p + dot32(x, e)
+    outs[1][here, :], outs[2][here, :] = loads_and_squares(
+        x, mine_ref[...], theirs_ref[...], l, q
+    )
+
+
+def fold(xs, e, at, cov, cat, sums, tile=512):
     pieces = len(xs)
     width, s = xs[0].shape
     genes = e.shape[1]
     covars = cov[0].shape[0]
     depth = pieces // 2 * s
-    blk = at * s // depth
-    assert blk * depth == at * s
+    blk = cat * s // depth
+    assert blk * depth == cat * s
     widths = (genes, covars, LANES)
     in_specs = [pl.BlockSpec((tile, s), lambda i: (i, 0))] * pieces + [HELD]
     in_specs += [pl.BlockSpec((covars, depth), lambda i: (0, blk))] * 2
@@ -225,15 +228,20 @@
     return high, mid, low
 
 
-def solve_kernel(mine_ref, theirs_ref, e_ref, o_ref):
-    size = mine_ref.shape[0]
-    n, genes = e_ref.shape
+def solve_kernel(*refs):
+    o_ref, e_ref = refs[-1], refs[-2]
+    size = refs[0].shape[0]
+    _, genes = e_ref.shape
     pitch = o_ref.shape[0] // 6
     across = (((1,), (1,)), ((), ()))
-    mine, theirs = mine_ref[...], theirs_ref[...]
-    m = lax.dot_general(mine, mine, across, preferred_element_type=jnp.float32)
-    m = m + lax.dot_general(theirs, theirs, across, preferred_element_type=jnp.float32)
-    cross = dot32(mine, e_ref[: n // 2, :]) + dot32(theirs, e_ref[n // 2 :, :])
+    m = jnp.zeros((size, size), jnp.float32)
+    cross = jnp.zeros((size, genes), jnp.float32)
+    first = 0
+    for c_ref in refs[:-2]:
+        c = c_ref[...]
+        m = m + lax.dot_general(c, c, across, preferred_element_type=jnp.float32)
+        cross = cross + dot32(c, e_ref[first : first + c.shape[1], :])
+        first += c.shape[1]
     line = lax.broadcasted_iota(jnp.int32, (size, size), 0)
     lane = lax.broadcasted_iota(jnp.int32, (size, size), 1)
     for k in range(size):
@@ -249,78 +257,94 @@
     down = (((0,), (0,)), ((), ()))
     slope = high(inverse, high(inverse, cross, (((1,), (0,)), ((), ()))), down)
     o_ref[...] = jnp.zeros(o_ref.shape, jnp.bfloat16)
-    for first, part in ((0, slope), (genes, inverse.T)):
+    for first, part in ((0, -slope), (genes, inverse.T)):
         h, i, l = thirds(part)
         for k, term in enumerate((h, i, l, h, i, h)):
             o_ref[k * pitch : k * pitch + size, first : first + part.shape[1]] = term
 
 
-def solve(cov, e):
-    size = cov[0].shape[0]
+def solve(covs, e):
+    size = covs[0].shape[0]
     pitch = size + -size % LANES
-    _, genes = e.shape
-    whole = lambda a: pl.BlockSpec(a.shape, lambda i: (0, 0))
-    table = jax.ShapeDtypeStruct((6 * pitch, genes + pitch), jnp.bfloat16)
+    genes = e.shape[1]
     return pl.pallas_call(
         solve_kernel,
         grid=(1,),
-        in_specs=[whole(cov[0]), whole(cov[1]), HELD],
-        out_specs=whole(table),
-        out_shape=table,
+        in_specs=[pl.BlockSpec(a.shape, lambda i: (0, 0)) for a in covs] + [HELD],
+        out_specs=HELD,
+        out_shape=pltpu.VMEM((6 * pitch, genes + pitch), jnp.bfloat16),
         compiler_params=limit(20),
         name="solve",
-    )(*cov, held(e))
-
-
-def finish_kernel(*refs, pieces, at, scale, start):
-    xs = refs[:pieces]
-    e_ref, mine_ref, theirs_ref, p_ref, l_ref, q_ref, d_ref, norm_ref = refs[pieces : pieces + 8]
-    o_ref = refs[-1]
-    tile, genes = o_ref.shape
-    here = pl.ds(pl.multiple_of(start + pl.program_id(0) * tile, tile), tile)
-    sums = tuple(r[here, :] for r in (p_ref, l_ref, q_ref))
-    p, l, q = fold_sums(xs, e_ref, mine_ref[...], theirs_ref[...], at, sums)
-    blank = -l.shape[1] % LANES
-    if blank:
-        l = jnp.concatenate([l, jnp.zeros((tile, blank), jnp.float32)], axis=1)
-    h, i, o = thirds(l)
-    t = dot32(jnp.concatenate([h, h, h, i, i, o], axis=1), d_ref[...])
-    w = t[:, genes:]
-    resid_norm = jnp.sum(q, axis=1, keepdims=True) - jnp.sum(w * w, axis=1, keepdims=True)
-    resid_norm = jnp.maximum(resid_norm, 0.0)
-    o_ref[...] = (
-        (p - t[:, :genes])
-        * (scale * lax.rsqrt(resid_norm + epsilon))
-        * lax.rsqrt(norm_ref[...] + epsilon)
-    )
-
-
-def finish(xs, e, cov, at, sums, d, norm, scale, start, block, blocks, out, tile=256):
-    pieces = len(xs)
+    )(*covs, held(e))
+
+
+def finish_kernel(*refs, sides, at, scale, starts, first):
+    p_ref, l_ref, q_ref, e_ref, mine_ref, theirs_ref, d_ref, norm_ref = refs[2 * sides : 2 * sides + 8]
+    out_ref, o_ref, sems = refs[-3:]
+    genes = o_ref.shape[1]
+    tile = refs[0].shape[0]
+    mine, theirs = mine_ref[...], theirs_ref[...]
+    gene_scale = scale * lax.rsqrt(norm_ref[...] + epsilon)
+    copies = []
+    for k in range(sides):
+        here = slice(starts[k], starts[k] + tile)
+        x, e = both_halves(refs[2 * k : 2 * k + 2], e_ref, at)
+        l, q = loads_and_squares(x, mine, theirs, l_ref[here, :], q_ref[here, :])
+        blank = -l.shape[1] % LANES
+        if blank:
+            l = jnp.concatenate([l, jnp.zeros((tile, blank), jnp.float32)], axis=1)
+        h, i, o = thirds(l)
+        l = jnp.concatenate([h, h, h, i, i, o], axis=1)
+        w = dot32(l, d_ref[:, genes:])
+        resid_norm = jnp.sum(q, axis=1, keepdims=True) - jnp.sum(w * w, axis=1, keepdims=True)
+        row_scale = lax.rsqrt(jnp.maximum(resid_norm, 0.0) + epsilon)
+        p = p_ref[here, :] + dot32(
+            jnp.concatenate([x, l], axis=1), jnp.concatenate([e, d_ref[:, :genes]], axis=0)
+        )
+        o_ref[k * tile : (k + 1) * tile, :] = p * row_scale * gene_scale
+        copies.append(
+            pltpu.make_async_copy(
+                o_ref.at[pl.ds(k * tile, tile), :],
+                out_ref.at[pl.ds(first + starts[k], tile), :],
+                sems.at[k],
+            )
+        )
+        copies[-1].start()
+    for copy in copies:
+        copy.wait()
+
+
+def finish(pieces, starts, e, at, cov, sums, d, norm, scale, block, blocks, out):
+    sides = len(pieces)
     width = sums[0].shape[0]
-    rows, s = xs[0].shape
+    tile, _ = pieces[0][0].shape
     genes = e.shape[1]
-    covars = cov[0].shape[0]
-    depth = pieces // 2 * s
-    blk = at * s // depth
-    assert blk * depth == at * s
     whole = lambda a: pl.BlockSpec(a.shape, lambda i: (0, 0))
-    in_specs = [pl.BlockSpec((tile, s), lambda i: (i, 0))] * pieces + [HELD]
-    in_specs += [pl.BlockSpec((covars, depth), lambda i: (0, blk))] * 2
-    in_specs += [HELD] * 3 + [whole(d), whole(norm)]
-    args = list(xs) + [held(e), *cov, *(held(a) for a in sums), d, norm]
+    args = [x for xs in pieces for x in xs]
+    in_specs = [whole(x) for x in args] + [HELD] * 4 + [whole(c) for c in cov] + [HELD, whole(norm)]
+    args += [*(held(a) for a in sums), held(e), *cov, held(d), norm]
     aliases = {}
     if out is not None:
-        in_specs.append(pl.BlockSpec(memory_space=pl.ANY))
+        in_specs.append(pl.BlockSpec(memory_space=pltpu.HBM))
         aliases = {len(args): 0}
         args.append(out)
-    first = (block * width + start) // tile
     return pl.pallas_call(
-        functools.partial(finish_kernel, pieces=pieces, at=at, scale=scale, start=start),
-        grid=(rows // tile,),
+        functools.partial(
+            finish_kernel,
+            sides=sides,
+            at=at,
+            scale=scale,
+            starts=starts,
+            first=block * width,
+        ),
+        grid=(1,),
         in_specs=in_specs,
-        out_specs=pl.BlockSpec((tile, genes), lambda i: (first + i, 0)),
+        out_specs=pl.BlockSpec(memory_space=pltpu.HBM),
         out_shape=jax.ShapeDtypeStruct((blocks * width, genes), jnp.float32),
+        scratch_shapes=[
+            pltpu.VMEM((sides * tile, genes), jnp.float32),
+            pltpu.SemaphoreType.DMA((sides,)),
+        ],
         input_output_aliases=aliases,
         compiler_params=limit(20),
         name="finish",
@@ -346,7 +370,7 @@
 def local(ring, dosage, covariates, expression, block_index, expr_row):
     blocks = block_index.shape[0]
     samples = expr_row.shape[0]
-    here, covars = covariates.shape
+    _, covars = covariates.shape
     scale = math.sqrt(samples - covars - 1)
     chips = len(ring)
     half = chips // 2
@@ -362,18 +386,18 @@
     def swap(x):
         return lax.ppermute(x, "samp", [(k, k ^ 1) for k in range(2 * chips)])
 
-    order = []
-    for d in range(1, half):
-        order += [d, -d]
-    order += [0, half]
+    rounds = [[1, -1, 0]] + [[d, -d] for d in range(2, half)] + [[half]]
+    order = sum(rounds, [])
 
     known = {0: covariates.T}
     for d in range(1, half + 1):
         known[d] = shift(known[d - 1], 1)
         if d < half:
             known[-d] = shift(known[1 - d], -1)
-    mine = jnp.concatenate([known[o] for o in order], axis=1)
-    cov = (mine, swap(mine))
+    covs = []
+    for d, some in enumerate(rounds, 1):
+        mine = jnp.concatenate([known[o] for o in some], axis=1)
+        covs.append((mine, swap(mine)))
 
     place = [0] * chips
     for k, chip in enumerate(ring):
@@ -387,12 +411,12 @@
     for b in range(blocks):
         picks.append(pick(dosage, block_index[b]))
     matched, panel_norm = match(expression, expr_row, table, me, chips)
-    back = solve(cov, matched)
+    back = solve([c[far] for far in range(2) for c in covs], matched)
 
     sums = []
     for b in range(blocks):
         other = swap(picks[b])
-        sums.append(fold([picks[b], other], matched, cov, 2 * half - 2, None))
+        sums.append(fold([picks[b], other], matched, 2, covs[0], 2, None))
     right = list(picks)
     left = list(picks)
     for d in range(1, half):
@@ -402,20 +426,30 @@
             near = swap(right[b])
             far = swap(left[b])
             pieces = [right[b], left[b], near, far]
-            sums[b] = fold(pieces, matched, cov, 2 * d - 2, sums[b])
+            if d == 1:
+                sums[b] = fold(pieces, matched, 0, covs[0], 0, sums[b])
+            else:
+                sums[b] = fold(pieces, matched, 2 * d - 1, covs[d - 1], 0, sums[b])
     width = picks[0].shape[0]
-    rows = width // PARTS
     out = None
-    for part in range(PARTS):
-        for b in range(blocks):
-            here = slice(part * rows, (part + 1) * rows)
-            last = shift(right[b][here], 1) if b % 2 == 0 else shift(left[b][here], -1)
-            other = swap(last)
+    for b in range(blocks):
+        parts = parts_of(b, blocks)
+        tile = width // (2 * parts)
+        for part in range(parts):
+            starts = [part * tile, width // 2 + part * tile]
+            pieces = []
+            for come, step, first in ((right, 1, starts[0]), (left, -1, starts[1])):
+                last = shift(come[b][first : first + tile], step)
+                pieces.append((last, swap(last)))
             out = finish(
-                [last, other], matched, cov, 2 * half - 1, sums[b], back, panel_norm,
-                scale, part * rows, b, blocks, out,
+                pieces, starts, matched, 2 * half - 1, covs[-1], sums[b], back, panel_norm,
+                scale, b, blocks, out,
             )
     return out
+
+
+def parts_of(b, blocks):
+    return PARTS if b == blocks - 1 else 1
 
 
 def solution(mesh):

time: 173 us -> 172 us (level)
  Pallas kernels: 61.3 us -> 51.9 us
  waiting for transfers between devices: 59.1 us -> 63.8 us
  starting transfers between devices: 33.8 us -> 37.1 us
    pallas_call x5 -> x3, Pallas kernels: 24 us -> 18.1 us  [the longest x1 9.3 us: solve(): pl.pallas_call(solve_kernel, grid=(1,), in_specs=[pl.BlockSpec(a.shape, l...]
    ppermute x23, waiting for transfers between devices: 59.1 us -> 63.1 us  [shift(): return lax.ppermute(x, 'samp', pairs)]
    pallas_call x8, Pallas kernels: 19 us -> 15.8 us  [fold(): pl.pallas_call(functools.partial(fold_kernel, pieces=pieces, at=at, fresh...]
    ppermute x23, starting transfers between devices: 29.4 us -> 32.3 us  [shift(): return lax.ppermute(x, 'samp', pairs)]
    unnamed x97 -> x92, local copies, waits for them, and re-layouts: 17 us -> 16.4 us
    ppermute x19 -> x22, starting transfers between devices: 4.44 us -> 4.84 us  [swap(): return lax.ppermute(x, 'samp', [(k, k ^ 1) for k in range(2 * chips)])]
  transfers between devices with their start and end apart: 42 -> 45, of which waited for: 16 -> 15; matrix products, arithmetic and copies ran while one was open for 1% -> 1% of each run, Pallas kernels for 33% -> 28%
where the time goes in v1:
time: 172 us
  waiting for transfers between devices  63.8 us (37%)
  Pallas kernels  51.9 us (30%)
  starting transfers between devices  37.1 us (22%)
  local copies, waits for them, and re-layouts  18.2 us (11%)
    ppermute x23, waiting for transfers between devices, shift(): return lax.ppermute(x, 'samp', pairs)  63.1 us
    ppermute x23, starting transfers between devices, shift(): return lax.ppermute(x, 'samp', pairs)  32.3 us
    unnamed x92, local copies, waits for them, and re-layouts  16.4 us
    pallas_call x8, Pallas kernels, fold(): pl.pallas_call(functools.partial(fold_kernel, pieces=pieces, at=at, fresh...  15.8 us
    pallas_call x1, Pallas kernels, solve(): pl.pallas_call(solve_kernel, grid=(1,), in_specs=[pl.BlockSpec(a.shape, l...  9.3 us
    pallas_call x2, Pallas kernels, pick(): pl.pallas_call(pick_kernel, grid_spec=pltpu.PrefetchScalarGridSpec(num_sc...  9.06 us
    pallas_call x1, Pallas kernels, match(): pl.pallas_call(functools.partial(match_kernel, chips=chips), grid_spec=pl...  9.03 us
    pallas_call x2, Pallas kernels, finish(): pl.pallas_call(functools.partial(finish_kernel, sides=sides, at=at, scale...  8.8 us
  transfers between devices with their start and end apart: 45, of which 15 were waited for; matrix products, arithmetic and copies ran while one was open for 1% of the time, Pallas kernels for 28%

profile of v1, /device:TPU:0, one launch (start us, length us, event | category | flops | bytes accessed | tf_op | source)
XLA Modules:
  0.0 171.9 jit_solution(17568285604808473055)
XLA Ops:
  0.0 3.1 %collective-permute-start.12 = (bf16[96,256]{1,0:T(8,128)(2,1)}, bf16[96,256]{1,0:T(8,128)(2,1)S(1)}, u32[]{:S(2)}, u32[]{:S(2)}) collective-permute-start(bf16[96,256]{1,0:T(8,128)(2,1)} %bitcast.6), channel_id=1, source_target_pairs={{0,4},{1,5},{4,8},{5,9},{8,12},{9,13},{12,14},{13,15},{14,10},{15,... | collective-permute-start | bytes 147464 | tf_op jit(solution)/shard_map/ppermute | solution.py:384
  3.9 4.5 %pick.3.refs_0_ = bf16[1024,256]{1,0:T(8,128)(2,1)S(1)} custom-call(s32[1024]{0:T(1024)S(1)} %bitcast.5, bf16[256,8192]{1,0:T(8,128)(2,1)} %x_hbm.3), custom_call_target="tpu_custom_call" | custom-call | tf_op jit(solution)/shard_map/pick/pallas_call | solution.py:72
  8.5 2.1 %collective-permute-start.28 = (bf16[1024,256]{1,0:T(8,128)(2,1)S(1)}, bf16[1024,256]{1,0:T(8,128)(2,1)S(1)}, u32[]{:S(2)}, u32[]{:S(2)}) collective-permute-start(bf16[1024,256]{1,0:T(8,128)(2,1)S(1)} %pick.3.refs_0_), channel_id=1, source_target_pairs={{0,4},{1,5},{4,8},{5,9},{8,12},{9,13},{12,14},{13,15},{14,10},{15,... | collective-permute-start | bytes 1572872 | tf_op jit(solution)/shard_map/ppermute | solution.py:384
  12.7 11.4 %collective-permute-done.13 = bf16[96,256]{1,0:T(8,128)(2,1)S(1)} collective-permute-done((bf16[96,256]{1,0:T(8,128)(2,1)S(1)}, bf16[96,256]{1,0:T(8,128)(2,1)S(1)}, u32[]{:S(2)}, u32[]{:S(2)}) %collective-permute-start.13) | collective-permute-done | bytes 49184 | tf_op jit(solution)/shard_map/ppermute | solution.py:384
  25.8 2.3 %collective-permute-done.16 = bf16[96,256]{1,0:T(8,128)(2,1)S(1)} collective-permute-done((bf16[96,256]{1,0:T(8,128)(2,1)S(1)}, bf16[96,256]{1,0:T(8,128)(2,1)S(1)}, u32[]{:S(2)}, u32[]{:S(2)}) %collective-permute-start.16) | collective-permute-done | bytes 49184 | tf_op jit(solution)/shard_map/ppermute | solution.py:384
  30.0 2.3 %collective-permute-done.14 = bf16[96,256]{1,0:T(8,128)(2,1)S(1)} collective-permute-done((bf16[96,256]{1,0:T(8,128)(2,1)S(1)}, bf16[96,256]{1,0:T(8,128)(2,1)S(1)}, u32[]{:S(2)}, u32[]{:S(2)}) %collective-permute-start.14) | collective-permute-done | bytes 49184 | tf_op jit(solution)/shard_map/ppermute | solution.py:384
  34.0 2.3 %collective-permute-done.17 = bf16[96,256]{1,0:T(8,128)(2,1)S(1)} collective-permute-done((bf16[96,256]{1,0:T(8,128)(2,1)S(1)}, bf16[96,256]{1,0:T(8,128)(2,1)S(1)}, u32[]{:S(2)}, u32[]{:S(2)}) %collective-permute-start.17) | collective-permute-done | bytes 49184 | tf_op jit(solution)/shard_map/ppermute | solution.py:384
  39.4 2.3 %collective-permute-done.26.refs_3_.refs_8_ = bf16[96,256]{1,0:T(8,128)(2,1)S(1)} collective-permute-done((bf16[96,256]{1,0:T(8,128)(2,1)S(1)}, bf16[96,256]{1,0:T(8,128)(2,1)S(1)}, u32[]{:S(2)}, u32[]{:S(2)}) %collective-permute-start.26) | collective-permute-done | bytes 49184 | tf_op jit(solution)/shard_map/ppermute | solution.py:384
  41.7 4.5 %pick.2.refs_0_ = bf16[1024,256]{1,0:T(8,128)(2,1)S(1)} custom-call(s32[1024]{0:T(1024)S(1)} %bitcast.4, bf16[256,8192]{1,0:T(8,128)(2,1)} %x_hbm.3), custom_call_target="tpu_custom_call" | custom-call | tf_op jit(solution)/shard_map/pick/pallas_call | solution.py:72
  53.7 8.0 %collective-permute-done.refs_0_ = bf16[1024,256]{1,0:T(8,128)(2,1)S(1)} collective-permute-done((bf16[1024,256]{1,0:T(8,128)(2,1)S(1)}, bf16[1024,256]{1,0:T(8,128)(2,1)S(1)}, u32[]{:S(2)}, u32[]{:S(2)}) %collective-permute-start) | collective-permute-done | bytes 524320 | tf_op jit(solution)/shard_map/ppermute | solution.py:384
  68.1 4.8 %collective-permute-done.29.refs_0_ = bf16[1024,256]{1,0:T(8,128)(2,1)S(1)} collective-permute-done((bf16[1024,256]{1,0:T(8,128)(2,1)S(1)}, bf16[1024,256]{1,0:T(8,128)(2,1)S(1)}, u32[]{:S(2)}, u32[]{:S(2)}) %collective-permute-start.29) | collective-permute-done | bytes 524320 | tf_op jit(solution)/shard_map/ppermute | solution.py:384
  79.2 4.9 %collective-permute-done.1.refs_0_ = bf16[1024,256]{1,0:T(8,128)(2,1)S(1)} collective-permute-done((bf16[1024,256]{1,0:T(8,128)(2,1)S(1)}, bf16[1024,256]{1,0:T(8,128)(2,1)S(1)}, u32[]{:S(2)}, u32[]{:S(2)}) %collective-permute-start.1) | collective-permute-done | bytes 524320 | tf_op jit(solution)/shard_map/ppermute | solution.py:384
  90.5 4.9 %collective-permute-done.30.refs_0_ = bf16[1024,256]{1,0:T(8,128)(2,1)S(1)} collective-permute-done((bf16[1024,256]{1,0:T(8,128)(2,1)S(1)}, bf16[1024,256]{1,0:T(8,128)(2,1)S(1)}, u32[]{:S(2)}, u32[]{:S(2)}) %collective-permute-start.30) | collective-permute-done | bytes 524320 | tf_op jit(solution)/shard_map/ppermute | solution.py:384
  98.8 7.8 %collective-permute-done.2.refs_0_ = bf16[1024,256]{1,0:T(8,128)(2,1)S(1)} collective-permute-done((bf16[1024,256]{1,0:T(8,128)(2,1)S(1)}, bf16[1024,256]{1,0:T(8,128)(2,1)S(1)}, u32[]{:S(2)}, u32[]{:S(2)}) %collective-permute-start.2) | collective-permute-done | bytes 524320 | tf_op jit(solution)/shard_map/ppermute | solution.py:384
  110.1 2.3 %collective-permute-done.31.refs_0_ = bf16[512,256]{1,0:T(8,128)(2,1)} collective-permute-done((bf16[512,256]{1,0:T(8,128)(2,1)S(1)}, bf16[512,256]{1,0:T(8,128)(2,1)}, u32[]{:S(2)}, u32[]{:S(2)}) %collective-permute-start.31) | collective-permute-done | bytes 262176 | tf_op jit(solution)/shard_map/ppermute | solution.py:384
  114.8 2.3 %collective-permute-done.3.refs_0_ = bf16[512,256]{1,0:T(8,128)(2,1)} collective-permute-done((bf16[512,256]{1,0:T(8,128)(2,1)S(1)}, bf16[512,256]{1,0:T(8,128)(2,1)}, u32[]{:S(2)}, u32[]{:S(2)}) %collective-permute-start.3) | collective-permute-done | bytes 262176 | tf_op jit(solution)/shard_map/ppermute | solution.py:384
  118.8 5.8 %collective-permute-done.8.refs_2_ = bf16[512,256]{1,0:T(8,128)(2,1)} collective-permute-done((bf16[512,256]{1,0:T(8,128)(2,1)S(1)}, bf16[512,256]{1,0:T(8,128)(2,1)}, u32[]{:S(2)}, u32[]{:S(2)}) %collective-permute-start.8) | collective-permute-done | bytes 262176 | tf_op jit(solution)/shard_map/ppermute | solution.py:384
  128.1 9.0 %match.1 = (bf16[4096,512]{1,0:T(8,128)(2,1)S(1)}, f32[1,512]{1,0:T(1,128)S(1)}) custom-call(s32[4096]{0:T(1024)S(1)} %copy-done.42, s32[24]{0:T(128)S(1)} %copy-done.43, s32[1]{0:T(128)} %bitcast.1.me_ref, bf16[4096,512]{1,0:T(8,128)(2,1)} %e_hbm.1), custom_call_target="tpu_custom_call" | custom-call | tf_op jit(solution)/shard_map/match/pallas_call | solution.py:135
  137.1 9.3 %solve.1.refs_10_ = bf16[768,640]{1,0:T(8,128)(2,1)S(1)} custom-call(bf16[96,768]{1,0:T(8,128)(2,1)S(1)} %pad_maximum_fusion.refs_3_.refs_5_.refs_0_, bf16[96,512]{1,0:T(8,128)(2,1)S(1)} %constant_dynamic-update-slice_fusion.2.refs_5_.refs_1_, bf16[96,512]{1,0:T(8,128)(2,1)S(1)} %constant_dynamic-update-slice_fusion.refs_5_.refs_2_, ...), custom_call_target="tpu_custom_call" | custom-call | tf_op jit(solution)/shard_map/solve/pallas_call | solution.py:270
  149.2 2.0 %fold.13 = (f32[1024,512]{1,0:T(8,128)S(1)}, f32[1024,96]{1,0:T(8,128)S(1)}, f32[1024,128]{1,0:T(8,128)S(1)}) custom-call(bf16[1024,256]{1,0:T(8,128)(2,1)S(1)} %copy-done.1, bf16[1024,256]{1,0:T(8,128)(2,1)S(1)} %copy-done.3, bf16[1024,256]{1,0:T(8,128)(2,1)S(1)} %copy-done.13, ...), custom_call_target="tpu_custom_call", output_to_operand_aliasing={{0}: (7, {}), {1}: (8, {}), {2}: (9, {})} | custom-call | tf_op jit(solution)/shard_map/fold/pallas_call | solution.py:211
  151.3 2.0 %fold.9 = (f32[1024,512]{1,0:T(8,128)S(1)}, f32[1024,96]{1,0:T(8,128)S(1)}, f32[1024,128]{1,0:T(8,128)S(1)}) custom-call(bf16[1024,256]{1,0:T(8,128)(2,1)S(1)} %copy-done.5, bf16[1024,256]{1,0:T(8,128)(2,1)S(1)} %copy-done.7, bf16[1024,256]{1,0:T(8,128)(2,1)S(1)} %copy-done.21, ...), custom_call_target="tpu_custom_call", output_to_operand_aliasing={{0}: (7, {}), {1}: (8, {}), {2}: (9, {})} | custom-call | tf_op jit(solution)/shard_map/fold/pallas_call | solution.py:211
  159.6 3.3 %fold.11 = (f32[1024,512]{1,0:T(8,128)S(1)}, f32[1024,96]{1,0:T(8,128)S(1)}, f32[1024,128]{1,0:T(8,128)S(1)}) custom-call(bf16[1024,256]{1,0:T(8,128)(2,1)S(1)} %collective-permute-done.2.refs_0_, bf16[1024,256]{1,0:T(8,128)(2,1)} %collective-permute-done.7.refs_1_, ...), custom_call_target="tpu_custom_call", output_to_operand_aliasing={{0}: (7, {}), {1}: (8, {}), {2}: (9, {})} | custom-call | tf_op jit(solution)/shard_map/fold/pallas_call | solution.py:211
  162.9 4.4 %finish.2.refs_12_ = f32[2048,512]{1,0:T(8,128)} custom-call(bf16[512,256]{1,0:T(8,128)(2,1)} %collective-permute-done.31.refs_0_, bf16[512,256]{1,0:T(8,128)(2,1)} %collective-permute-done.32.refs_1_, bf16[512,256]{1,0:T(8,128)(2,1)} %collective-permute-done.36.refs_2_, bf16[512,256]{1,0:T(8,128)(2,1)} %collective-permute-done.37.refs_3_, ...), custom_call_target="tpu_custom_call" | custom-call | tf_op jit(solution)/shard_map/finish/pallas_call | solution.py:331
  167.4 4.4 %finish.3 = f32[2048,512]{1,0:T(8,128)} custom-call(bf16[512,256]{1,0:T(8,128)(2,1)} %collective-permute-done.3.refs_0_, bf16[512,256]{1,0:T(8,128)(2,1)} %collective-permute-done.4.refs_1_, bf16[512,256]{1,0:T(8,128)(2,1)} %collective-permute-done.8.refs_2_, bf16[512,256]{1,0:T(8,128)(2,1)} %collective-permute-done.9.refs_3_, ...), custom_call_target="tpu_custom_call", output_to_operand_aliasing={{}: (12, {})} | custom-call | tf_op jit(solution)/shard_map/finish/pallas_call | solution.py:331
  (180 shorter events, 60.9 us)
Async XLA Ops:
  8.4 40.3 %collective-permute-start.44 = (bf16[1024,256]{1,0:T(8,128)(2,1)S(1)}, bf16[1024,256]{1,0:T(8,128)(2,1)S(1)}, u32[]{:S(2)}, u32[]{:S(2)}) collective-permute-start(bf16[1024,256]{1,0:T(8,128)(2,1)S(1)} %pick.3.refs_0_), channel_id=1, source_target_pairs={{0,1},{1,0},{2,3},{3,2},{4,5},{5,4},{6,7},{7,6},{8,9},{9,8},{10,11... | collective-permute-start | bytes 1572872 | tf_op jit(solution)/shard_map/ppermute | solution.py:387
  8.5 41.3 %collective-permute-start.28 = (bf16[1024,256]{1,0:T(8,128)(2,1)S(1)}, bf16[1024,256]{1,0:T(8,128)(2,1)S(1)}, u32[]{:S(2)}, u32[]{:S(2)}) collective-permute-start(bf16[1024,256]{1,0:T(8,128)(2,1)S(1)} %pick.3.refs_0_), channel_id=1, source_target_pairs={{0,4},{1,5},{4,8},{5,9},{8,12},{9,13},{12,14},{13,15},{14,10},{15,... | collective-permute-start | bytes 1572872 | tf_op jit(solution)/shard_map/ppermute | solution.py:384
  10.5 39.2 %collective-permute-start.33 = (bf16[1024,256]{1,0:T(8,128)(2,1)S(1)}, bf16[1024,256]{1,0:T(8,128)(2,1)S(1)}, u32[]{:S(2)}, u32[]{:S(2)}) collective-permute-start(bf16[1024,256]{1,0:T(8,128)(2,1)S(1)} %pick.3.refs_0_), channel_id=1, source_target_pairs={{0,2},{1,3},{4,0},{5,1},{8,4},{9,5},{12,8},{13,9},{14,12},{15,13},... | collective-permute-start | bytes 1572872 | tf_op jit(solution)/shard_map/ppermute | solution.py:384
  12.6 23.8 %collective-permute-start.24 = (bf16[96,768]{1,0:T(8,128)(2,1)S(1)}, bf16[96,768]{1,0:T(8,128)(2,1)S(1)}, u32[]{:S(2)}, u32[]{:S(2)}) collective-permute-start(bf16[96,768]{1,0:T(8,128)(2,1)S(1)} %pad_maximum_fusion.refs_3_.refs_5_.refs_0_), channel_id=1, source_target_pairs={{0,1},{1,0},{2,3},{3,2},{4,5},{5,4},{6,7},{7,6},{8,9},{9,8},{10,11... | collective-permute-start | bytes 442376 | tf_op jit(solution)/shard_map/ppermute | solution.py:387
  46.9 14.8 %collective-permute-start = (bf16[1024,256]{1,0:T(8,128)(2,1)S(1)}, bf16[1024,256]{1,0:T(8,128)(2,1)S(1)}, u32[]{:S(2)}, u32[]{:S(2)}) collective-permute-start(bf16[1024,256]{1,0:T(8,128)(2,1)S(1)} %pick.2.refs_0_), channel_id=1, source_target_pairs={{0,4},{1,5},{4,8},{5,9},{8,12},{9,13},{12,14},{13,15},{14,10},{15,... | collective-permute-start | bytes 1572872 | tf_op jit(solution)/shard_map/ppermute | solution.py:384
  49.5 14.7 %collective-permute-start.5 = (bf16[1024,256]{1,0:T(8,128)(2,1)S(1)}, bf16[1024,256]{1,0:T(8,128)(2,1)S(1)}, u32[]{:S(2)}, u32[]{:S(2)}) collective-permute-start(bf16[1024,256]{1,0:T(8,128)(2,1)S(1)} %pick.2.refs_0_), channel_id=1, source_target_pairs={{0,2},{1,3},{4,0},{5,1},{8,4},{9,5},{12,8},{13,9},{14,12},{15,13},... | collective-permute-start | bytes 1572872 | tf_op jit(solution)/shard_map/ppermute | solution.py:384
  49.8 14.4 %collective-permute-start.42 = (bf16[1024,256]{1,0:T(8,128)(2,1)S(1)}, bf16[1024,256]{1,0:T(8,128)(2,1)S(1)}, u32[]{:S(2)}, u32[]{:S(2)}) collective-permute-start(bf16[1024,256]{1,0:T(8,128)(2,1)S(1)} %collective-permute-done.28.refs_0_), channel_id=1, source_target_pairs={{0,1},{1,0},{2,3},{3,2},{4,5},{5,4},{6,7},{7,6},{8,9},{9,8},{10,11... | collective-permute-start | bytes 1572872 | tf_op jit(solution)/shard_map/ppermute | solution.py:387
  49.8 15.8 %collective-permute-start.43 = (bf16[1024,256]{1,0:T(8,128)(2,1)S(1)}, bf16[1024,256]{1,0:T(8,128)(2,1)S(1)}, u32[]{:S(2)}, u32[]{:S(2)}) collective-permute-start(bf16[1024,256]{1,0:T(8,128)(2,1)S(1)} %collective-permute-done.33.refs_1_), channel_id=1, source_target_pairs={{0,1},{1,0},{2,3},{3,2},{4,5},{5,4},{6,7},{7,6},{8,9},{9,8},{10,11... | collective-permute-start | bytes 1572872 | tf_op jit(solution)/shard_map/ppermute | solution.py:387
  51.1 21.8 %collective-permute-start.29 = (bf16[1024,256]{1,0:T(8,128)(2,1)S(1)}, bf16[1024,256]{1,0:T(8,128)(2,1)S(1)}, u32[]{:S(2)}, u32[]{:S(2)}) collective-permute-start(bf16[1024,256]{1,0:T(8,128)(2,1)S(1)} %collective-permute-done.28.refs_0_), channel_id=1, source_target_pairs={{0,4},{1,5},{4,8},{5,9},{8,12},{9,13},{12,14},{13,15},{14,10},{15,... | collective-permute-start | bytes 1572872 | tf_op jit(solution)/shard_map/ppermute | solution.py:384
  66.4 17.8 %collective-permute-start.1 = (bf16[1024,256]{1,0:T(8,128)(2,1)S(1)}, bf16[1024,256]{1,0:T(8,128)(2,1)S(1)}, u32[]{:S(2)}, u32[]{:S(2)}) collective-permute-start(bf16[1024,256]{1,0:T(8,128)(2,1)S(1)} %collective-permute-done.refs_0_), channel_id=1, source_target_pairs={{0,4},{1,5},{4,8},{5,9},{8,12},{9,13},{12,14},{13,15},{14,10},{15,... | collective-permute-start | bytes 1572872 | tf_op jit(solution)/shard_map/ppermute | solution.py:384
  77.6 17.8 %collective-permute-start.30 = (bf16[1024,256]{1,0:T(8,128)(2,1)S(1)}, bf16[1024,256]{1,0:T(8,128)(2,1)S(1)}, u32[]{:S(2)}, u32[]{:S(2)}) collective-permute-start(bf16[1024,256]{1,0:T(8,128)(2,1)S(1)} %collective-permute-done.29.refs_0_), channel_id=1, source_target_pairs={{0,4},{1,5},{4,8},{5,9},{8,12},{9,13},{12,14},{13,15},{14,10},{15,... | collective-permute-start | bytes 1572872 | tf_op jit(solution)/shard_map/ppermute | solution.py:384
  86.7 19.9 %collective-permute-start.2 = (bf16[1024,256]{1,0:T(8,128)(2,1)S(1)}, bf16[1024,256]{1,0:T(8,128)(2,1)S(1)}, u32[]{:S(2)}, u32[]{:S(2)}) collective-permute-start(bf16[1024,256]{1,0:T(8,128)(2,1)S(1)} %collective-permute-done.1.refs_0_), channel_id=1, source_target_pairs={{0,4},{1,5},{4,8},{5,9},{8,12},{9,13},{12,14},{13,15},{14,10},{15,... | collective-permute-start | bytes 1572872 | tf_op jit(solution)/shard_map/ppermute | solution.py:384
  88.3 20.0 %collective-permute-start.19 = (bf16[1024,256]{1,0:T(8,128)(2,1)S(1)}, bf16[1024,256]{1,0:T(8,128)(2,1)S(1)}, u32[]{:S(2)}, u32[]{:S(2)}) collective-permute-start(bf16[1024,256]{1,0:T(8,128)(2,1)S(1)} %collective-permute-done.1.refs_0_), channel_id=1, source_target_pairs={{0,1},{1,0},{2,3},{3,2},{4,5},{5,4},{6,7},{7,6},{8,9},{9,8},{10,11... | collective-permute-start | bytes 1572872 | tf_op jit(solution)/shard_map/ppermute | solution.py:387
  90.0 18.8 %collective-permute-start.20 = (bf16[1024,256]{1,0:T(8,128)(2,1)S(1)}, bf16[1024,256]{1,0:T(8,128)(2,1)S(1)}, u32[]{:S(2)}, u32[]{:S(2)}) collective-permute-start(bf16[1024,256]{1,0:T(8,128)(2,1)S(1)} %collective-permute-done.6.refs_1_), channel_id=1, source_target_pairs={{0,1},{1,0},{2,3},{3,2},{4,5},{5,4},{6,7},{7,6},{8,9},{9,8},{10,11... | collective-permute-start | bytes 1572872 | tf_op jit(solution)/shard_map/ppermute | solution.py:387
  95.4 14.2 %collective-permute-start.7 = (bf16[1024,256]{1,0:T(8,128)(2,1)S(1)}, bf16[1024,256]{1,0:T(8,128)(2,1)}, u32[]{:S(2)}, u32[]{:S(2)}) collective-permute-start(bf16[1024,256]{1,0:T(8,128)(2,1)S(1)} %collective-permute-done.6.refs_1_), channel_id=1, source_target_pairs={{0,2},{1,3},{4,0},{5,1},{8,4},{9,5},{12,8},{13,9},{14,12},{15,13},... | collective-permute-start | bytes 1572872 | tf_op jit(solution)/shard_map/ppermute | solution.py:384
  97.9 14.4 %collective-permute-start.31 = (bf16[512,256]{1,0:T(8,128)(2,1)S(1)}, bf16[512,256]{1,0:T(8,128)(2,1)}, u32[]{:S(2)}, u32[]{:S(2)}) collective-permute-start(bf16[512,256]{1,0:T(8,128)(2,1)S(1)} %slice.26), channel_id=1, source_target_pairs={{0,4},{1,5},{4,8},{5,9},{8,12},{9,13},{12,14},{13,15},{14,10},{15,... | collective-permute-start | bytes 786440 | tf_op jit(solution)/shard_map/ppermute | solution.py:384
  109.5 15.1 %collective-permute-start.38 = (bf16[1024,256]{1,0:T(8,128)(2,1)S(1)}, bf16[1024,256]{1,0:T(8,128)(2,1)S(1)}, u32[]{:S(2)}, u32[]{:S(2)}) collective-permute-start(bf16[1024,256]{1,0:T(8,128)(2,1)S(1)} %collective-permute-done.30.refs_0_), channel_id=1, source_target_pairs={{0,1},{1,0},{2,3},{3,2},{4,5},{5,4},{6,7},{7,6},{8,9},{9,8},{10,11... | collective-permute-start | bytes 1572872 | tf_op jit(solution)/shard_map/ppermute | solution.py:387
  109.5 16.4 %collective-permute-start.39 = (bf16[1024,256]{1,0:T(8,128)(2,1)S(1)}, bf16[1024,256]{1,0:T(8,128)(2,1)S(1)}, u32[]{:S(2)}, u32[]{:S(2)}) collective-permute-start(bf16[1024,256]{1,0:T(8,128)(2,1)S(1)} %collective-permute-done.35.refs_1_), channel_id=1, source_target_pairs={{0,1},{1,0},{2,3},{3,2},{4,5},{5,4},{6,7},{7,6},{8,9},{9,8},{10,11... | collective-permute-start | bytes 1572872 | tf_op jit(solution)/shard_map/ppermute | solution.py:387
  112.3 14.4 %collective-permute-start.10 = (bf16[1024,256]{1,0:T(8,128)(2,1)S(1)}, bf16[1024,256]{1,0:T(8,128)(2,1)S(1)}, u32[]{:S(2)}, u32[]{:S(2)}) collective-permute-start(bf16[1024,256]{1,0:T(8,128)(2,1)S(1)} %collective-permute-done.2.refs_0_), channel_id=1, source_target_pairs={{0,1},{1,0},{2,3},{3,2},{4,5},{5,4},{6,7},{7,6},{8,9},{9,8},{10,11... | collective-permute-start | bytes 1572872 | tf_op jit(solution)/shard_map/ppermute | solution.py:387
  113.8 45.8 %collective-permute-start.11 = (bf16[1024,256]{1,0:T(8,128)(2,1)}, bf16[1024,256]{1,0:T(8,128)(2,1)}, u32[]{:S(2)}, u32[]{:S(2)}) collective-permute-start(bf16[1024,256]{1,0:T(8,128)(2,1)} %collective-permute-done.7.refs_1_), channel_id=1, source_target_pairs={{0,1},{1,0},{2,3},{3,2},{4,5},{5,4},{6,7},{7,6},{8,9},{9,8},{10,11... | collective-permute-start | bytes 1572872 | tf_op jit(solution)/shard_map/ppermute | solution.py:387
  124.7 38.3 %collective-permute-start.32 = (bf16[512,256]{1,0:T(8,128)(2,1)}, bf16[512,256]{1,0:T(8,128)(2,1)}, u32[]{:S(2)}, u32[]{:S(2)}) collective-permute-start(bf16[512,256]{1,0:T(8,128)(2,1)} %collective-permute-done.31.refs_0_), channel_id=1, source_target_pairs={{0,1},{1,0},{2,3},{3,2},{4,5},{5,4},{6,7},{7,6},{8,9},{9,8},{10,11... | collective-permute-start | bytes 786440 | tf_op jit(solution)/shard_map/ppermute | solution.py:387
  125.5 37.5 %collective-permute-start.37 = (bf16[512,256]{1,0:T(8,128)(2,1)}, bf16[512,256]{1,0:T(8,128)(2,1)}, u32[]{:S(2)}, u32[]{:S(2)}) collective-permute-start(bf16[512,256]{1,0:T(8,128)(2,1)} %collective-permute-done.36.refs_2_), channel_id=1, source_target_pairs={{0,1},{1,0},{2,3},{3,2},{4,5},{5,4},{6,7},{7,6},{8,9},{9,8},{10,11... | collective-permute-start | bytes 786440 | tf_op jit(solution)/shard_map/ppermute | solution.py:387
  126.8 40.6 %collective-permute-start.4 = (bf16[512,256]{1,0:T(8,128)(2,1)}, bf16[512,256]{1,0:T(8,128)(2,1)}, u32[]{:S(2)}, u32[]{:S(2)}) collective-permute-start(bf16[512,256]{1,0:T(8,128)(2,1)} %collective-permute-done.3.refs_0_), channel_id=1, source_target_pairs={{0,1},{1,0},{2,3},{3,2},{4,5},{5,4},{6,7},{7,6},{8,9},{9,8},{10,11... | collective-permute-start | bytes 786440 | tf_op jit(solution)/shard_map/ppermute | solution.py:387
  127.6 39.8 %collective-permute-start.9 = (bf16[512,256]{1,0:T(8,128)(2,1)}, bf16[512,256]{1,0:T(8,128)(2,1)}, u32[]{:S(2)}, u32[]{:S(2)}) collective-permute-start(bf16[512,256]{1,0:T(8,128)(2,1)} %collective-permute-done.8.refs_2_), channel_id=1, source_target_pairs={{0,1},{1,0},{2,3},{3,2},{4,5},{5,4},{6,7},{7,6},{8,9},{9,8},{10,11... | collective-permute-start | bytes 786440 | tf_op jit(solution)/shard_map/ppermute | solution.py:387
  (66 other events, 436.6 us)

commit v2 on v1

--- a/solution.py
+++ b/solution.py
@@ -433,7 +433,7 @@
     width = picks[0].shape[0]
     out = None
     for b in range(blocks):
-        parts = parts_of(b, blocks)
+        parts = parts_of()
         tile = width // (2 * parts)
         for part in range(parts):
             starts = [part * tile, width // 2 + part * tile]
@@ -448,8 +448,8 @@
     return out
 
 
-def parts_of(b, blocks):
-    return PARTS if b == blocks - 1 else 1
+def parts_of():
+    return PARTS
 
 
 def solution(mesh):

time: 172 us -> 172 us (level)
  no operation moved by 1% of the time
where the time goes in v2:
time: 172 us
  waiting for transfers between devices  63.8 us (37%)
  Pallas kernels  51.9 us (30%)
  starting transfers between devices  37.1 us (22%)
  local copies, waits for them, and re-layouts  18.2 us (11%)
    ppermute x23, waiting for transfers between devices, shift(): return lax.ppermute(x, 'samp', pairs)  63.1 us
    ppermute x23, starting transfers between devices, shift(): return lax.ppermute(x, 'samp', pairs)  32.3 us
    unnamed x92, local copies, waits for them, and re-layouts  16.4 us
    pallas_call x8, Pallas kernels, fold(): pl.pallas_call(functools.partial(fold_kernel, pieces=pieces, at=at, fresh...  15.8 us
    pallas_call x1, Pallas kernels, solve(): pl.pallas_call(solve_kernel, grid=(1,), in_specs=[pl.BlockSpec(a.shape, l...  9.3 us
    pallas_call x2, Pallas kernels, pick(): pl.pallas_call(pick_kernel, grid_spec=pltpu.PrefetchScalarGridSpec(num_sc...  9.06 us
    pallas_call x1, Pallas kernels, match(): pl.pallas_call(functools.partial(match_kernel, chips=chips), grid_spec=pl...  9.03 us
    pallas_call x2, Pallas kernels, finish(): pl.pallas_call(functools.partial(finish_kernel, sides=sides, at=at, scale...  8.8 us
  transfers between devices with their start and end apart: 45, of which 15 were waited for; matrix products, arithmetic and copies ran while one was open for 1% of the time, Pallas kernels for 28%

profile of v2, /device:TPU:0, one launch (start us, length us, event | category | flops | bytes accessed | tf_op | source)
XLA Modules:
  0.0 171.9 jit_solution(17568285604808473055)
XLA Ops:
  0.0 3.1 %collective-permute-start.12 = (bf16[96,256]{1,0:T(8,128)(2,1)}, bf16[96,256]{1,0:T(8,128)(2,1)S(1)}, u32[]{:S(2)}, u32[]{:S(2)}) collective-permute-start(bf16[96,256]{1,0:T(8,128)(2,1)} %bitcast.6), channel_id=1, source_target_pairs={{0,4},{1,5},{4,8},{5,9},{8,12},{9,13},{12,14},{13,15},{14,10},{15,... | collective-permute-start | bytes 147464 | tf_op jit(solution)/shard_map/ppermute | solution.py:384
  3.9 4.5 %pick.3.refs_0_ = bf16[1024,256]{1,0:T(8,128)(2,1)S(1)} custom-call(s32[1024]{0:T(1024)S(1)} %bitcast.5, bf16[256,8192]{1,0:T(8,128)(2,1)} %x_hbm.3), custom_call_target="tpu_custom_call" | custom-call | tf_op jit(solution)/shard_map/pick/pallas_call | solution.py:72
  8.5 2.1 %collective-permute-start.28 = (bf16[1024,256]{1,0:T(8,128)(2,1)S(1)}, bf16[1024,256]{1,0:T(8,128)(2,1)S(1)}, u32[]{:S(2)}, u32[]{:S(2)}) collective-permute-start(bf16[1024,256]{1,0:T(8,128)(2,1)S(1)} %pick.3.refs_0_), channel_id=1, source_target_pairs={{0,4},{1,5},{4,8},{5,9},{8,12},{9,13},{12,14},{13,15},{14,10},{15,... | collective-permute-start | bytes 1572872 | tf_op jit(solution)/shard_map/ppermute | solution.py:384
  12.7 11.4 %collective-permute-done.13 = bf16[96,256]{1,0:T(8,128)(2,1)S(1)} collective-permute-done((bf16[96,256]{1,0:T(8,128)(2,1)S(1)}, bf16[96,256]{1,0:T(8,128)(2,1)S(1)}, u32[]{:S(2)}, u32[]{:S(2)}) %collective-permute-start.13) | collective-permute-done | bytes 49184 | tf_op jit(solution)/shard_map/ppermute | solution.py:384
  25.8 2.3 %collective-permute-done.16 = bf16[96,256]{1,0:T(8,128)(2,1)S(1)} collective-permute-done((bf16[96,256]{1,0:T(8,128)(2,1)S(1)}, bf16[96,256]{1,0:T(8,128)(2,1)S(1)}, u32[]{:S(2)}, u32[]{:S(2)}) %collective-permute-start.16) | collective-permute-done | bytes 49184 | tf_op jit(solution)/shard_map/ppermute | solution.py:384
  30.0 2.3 %collective-permute-done.14 = bf16[96,256]{1,0:T(8,128)(2,1)S(1)} collective-permute-done((bf16[96,256]{1,0:T(8,128)(2,1)S(1)}, bf16[96,256]{1,0:T(8,128)(2,1)S(1)}, u32[]{:S(2)}, u32[]{:S(2)}) %collective-permute-start.14) | collective-permute-done | bytes 49184 | tf_op jit(solution)/shard_map/ppermute | solution.py:384
  34.0 2.3 %collective-permute-done.17 = bf16[96,256]{1,0:T(8,128)(2,1)S(1)} collective-permute-done((bf16[96,256]{1,0:T(8,128)(2,1)S(1)}, bf16[96,256]{1,0:T(8,128)(2,1)S(1)}, u32[]{:S(2)}, u32[]{:S(2)}) %collective-permute-start.17) | collective-permute-done | bytes 49184 | tf_op jit(solution)/shard_map/ppermute | solution.py:384
  39.4 2.3 %collective-permute-done.26.refs_3_.refs_8_ = bf16[96,256]{1,0:T(8,128)(2,1)S(1)} collective-permute-done((bf16[96,256]{1,0:T(8,128)(2,1)S(1)}, bf16[96,256]{1,0:T(8,128)(2,1)S(1)}, u32[]{:S(2)}, u32[]{:S(2)}) %collective-permute-start.26) | collective-permute-done | bytes 49184 | tf_op jit(solution)/shard_map/ppermute | solution.py:384
  41.7 4.5 %pick.2.refs_0_ = bf16[1024,256]{1,0:T(8,128)(2,1)S(1)} custom-call(s32[1024]{0:T(1024)S(1)} %bitcast.4, bf16[256,8192]{1,0:T(8,128)(2,1)} %x_hbm.3), custom_call_target="tpu_custom_call" | custom-call | tf_op jit(solution)/shard_map/pick/pallas_call | solution.py:72
  53.7 8.0 %collective-permute-done.refs_0_ = bf16[1024,256]{1,0:T(8,128)(2,1)S(1)} collective-permute-done((bf16[1024,256]{1,0:T(8,128)(2,1)S(1)}, bf16[1024,256]{1,0:T(8,128)(2,1)S(1)}, u32[]{:S(2)}, u32[]{:S(2)}) %collective-permute-start) | collective-permute-done | bytes 524320 | tf_op jit(solution)/shard_map/ppermute | solution.py:384
  68.1 4.8 %collective-permute-done.29.refs_0_ = bf16[1024,256]{1,0:T(8,128)(2,1)S(1)} collective-permute-done((bf16[1024,256]{1,0:T(8,128)(2,1)S(1)}, bf16[1024,256]{1,0:T(8,128)(2,1)S(1)}, u32[]{:S(2)}, u32[]{:S(2)}) %collective-permute-start.29) | collective-permute-done | bytes 524320 | tf_op jit(solution)/shard_map/ppermute | solution.py:384
  79.2 4.9 %collective-permute-done.1.refs_0_ = bf16[1024,256]{1,0:T(8,128)(2,1)S(1)} collective-permute-done((bf16[1024,256]{1,0:T(8,128)(2,1)S(1)}, bf16[1024,256]{1,0:T(8,128)(2,1)S(1)}, u32[]{:S(2)}, u32[]{:S(2)}) %collective-permute-start.1) | collective-permute-done | bytes 524320 | tf_op jit(solution)/shard_map/ppermute | solution.py:384
  90.5 4.9 %collective-permute-done.30.refs_0_ = bf16[1024,256]{1,0:T(8,128)(2,1)S(1)} collective-permute-done((bf16[1024,256]{1,0:T(8,128)(2,1)S(1)}, bf16[1024,256]{1,0:T(8,128)(2,1)S(1)}, u32[]{:S(2)}, u32[]{:S(2)}) %collective-permute-start.30) | collective-permute-done | bytes 524320 | tf_op jit(solution)/shard_map/ppermute | solution.py:384
  98.8 7.8 %collective-permute-done.2.refs_0_ = bf16[1024,256]{1,0:T(8,128)(2,1)S(1)} collective-permute-done((bf16[1024,256]{1,0:T(8,128)(2,1)S(1)}, bf16[1024,256]{1,0:T(8,128)(2,1)S(1)}, u32[]{:S(2)}, u32[]{:S(2)}) %collective-permute-start.2) | collective-permute-done | bytes 524320 | tf_op jit(solution)/shard_map/ppermute | solution.py:384
  110.1 2.3 %collective-permute-done.31.refs_0_ = bf16[512,256]{1,0:T(8,128)(2,1)} collective-permute-done((bf16[512,256]{1,0:T(8,128)(2,1)S(1)}, bf16[512,256]{1,0:T(8,128)(2,1)}, u32[]{:S(2)}, u32[]{:S(2)}) %collective-permute-start.31) | collective-permute-done | bytes 262176 | tf_op jit(solution)/shard_map/ppermute | solution.py:384
  114.8 2.3 %collective-permute-done.3.refs_0_ = bf16[512,256]{1,0:T(8,128)(2,1)} collective-permute-done((bf16[512,256]{1,0:T(8,128)(2,1)S(1)}, bf16[512,256]{1,0:T(8,128)(2,1)}, u32[]{:S(2)}, u32[]{:S(2)}) %collective-permute-start.3) | collective-permute-done | bytes 262176 | tf_op jit(solution)/shard_map/ppermute | solution.py:384
  118.8 5.8 %collective-permute-done.8.refs_2_ = bf16[512,256]{1,0:T(8,128)(2,1)} collective-permute-done((bf16[512,256]{1,0:T(8,128)(2,1)S(1)}, bf16[512,256]{1,0:T(8,128)(2,1)}, u32[]{:S(2)}, u32[]{:S(2)}) %collective-permute-start.8) | collective-permute-done | bytes 262176 | tf_op jit(solution)/shard_map/ppermute | solution.py:384
  128.1 9.0 %match.1 = (bf16[4096,512]{1,0:T(8,128)(2,1)S(1)}, f32[1,512]{1,0:T(1,128)S(1)}) custom-call(s32[4096]{0:T(1024)S(1)} %copy-done.42, s32[24]{0:T(128)S(1)} %copy-done.43, s32[1]{0:T(128)} %bitcast.1.me_ref, bf16[4096,512]{1,0:T(8,128)(2,1)} %e_hbm.1), custom_call_target="tpu_custom_call" | custom-call | tf_op jit(solution)/shard_map/match/pallas_call | solution.py:135
  137.1 9.3 %solve.1.refs_10_ = bf16[768,640]{1,0:T(8,128)(2,1)S(1)} custom-call(bf16[96,768]{1,0:T(8,128)(2,1)S(1)} %pad_maximum_fusion.refs_3_.refs_5_.refs_0_, bf16[96,512]{1,0:T(8,128)(2,1)S(1)} %constant_dynamic-update-slice_fusion.2.refs_5_.refs_1_, bf16[96,512]{1,0:T(8,128)(2,1)S(1)} %constant_dynamic-update-slice_fusion.refs_5_.refs_2_, ...), custom_call_target="tpu_custom_call" | custom-call | tf_op jit(solution)/shard_map/solve/pallas_call | solution.py:270
  149.2 2.0 %fold.13 = (f32[1024,512]{1,0:T(8,128)S(1)}, f32[1024,96]{1,0:T(8,128)S(1)}, f32[1024,128]{1,0:T(8,128)S(1)}) custom-call(bf16[1024,256]{1,0:T(8,128)(2,1)S(1)} %copy-done.1, bf16[1024,256]{1,0:T(8,128)(2,1)S(1)} %copy-done.3, bf16[1024,256]{1,0:T(8,128)(2,1)S(1)} %copy-done.13, ...), custom_call_target="tpu_custom_call", output_to_operand_aliasing={{0}: (7, {}), {1}: (8, {}), {2}: (9, {})} | custom-call | tf_op jit(solution)/shard_map/fold/pallas_call | solution.py:211
  151.3 2.0 %fold.9 = (f32[1024,512]{1,0:T(8,128)S(1)}, f32[1024,96]{1,0:T(8,128)S(1)}, f32[1024,128]{1,0:T(8,128)S(1)}) custom-call(bf16[1024,256]{1,0:T(8,128)(2,1)S(1)} %copy-done.5, bf16[1024,256]{1,0:T(8,128)(2,1)S(1)} %copy-done.7, bf16[1024,256]{1,0:T(8,128)(2,1)S(1)} %copy-done.21, ...), custom_call_target="tpu_custom_call", output_to_operand_aliasing={{0}: (7, {}), {1}: (8, {}), {2}: (9, {})} | custom-call | tf_op jit(solution)/shard_map/fold/pallas_call | solution.py:211
  159.6 3.3 %fold.11 = (f32[1024,512]{1,0:T(8,128)S(1)}, f32[1024,96]{1,0:T(8,128)S(1)}, f32[1024,128]{1,0:T(8,128)S(1)}) custom-call(bf16[1024,256]{1,0:T(8,128)(2,1)S(1)} %collective-permute-done.2.refs_0_, bf16[1024,256]{1,0:T(8,128)(2,1)} %collective-permute-done.7.refs_1_, ...), custom_call_target="tpu_custom_call", output_to_operand_aliasing={{0}: (7, {}), {1}: (8, {}), {2}: (9, {})} | custom-call | tf_op jit(solution)/shard_map/fold/pallas_call | solution.py:211
  162.9 4.4 %finish.2.refs_12_ = f32[2048,512]{1,0:T(8,128)} custom-call(bf16[512,256]{1,0:T(8,128)(2,1)} %collective-permute-done.31.refs_0_, bf16[512,256]{1,0:T(8,128)(2,1)} %collective-permute-done.32.refs_1_, bf16[512,256]{1,0:T(8,128)(2,1)} %collective-permute-done.36.refs_2_, bf16[512,256]{1,0:T(8,128)(2,1)} %collective-permute-done.37.refs_3_, ...), custom_call_target="tpu_custom_call" | custom-call | tf_op jit(solution)/shard_map/finish/pallas_call | solution.py:331
  167.4 4.4 %finish.3 = f32[2048,512]{1,0:T(8,128)} custom-call(bf16[512,256]{1,0:T(8,128)(2,1)} %collective-permute-done.3.refs_0_, bf16[512,256]{1,0:T(8,128)(2,1)} %collective-permute-done.4.refs_1_, bf16[512,256]{1,0:T(8,128)(2,1)} %collective-permute-done.8.refs_2_, bf16[512,256]{1,0:T(8,128)(2,1)} %collective-permute-done.9.refs_3_, ...), custom_call_target="tpu_custom_call", output_to_operand_aliasing={{}: (12, {})} | custom-call | tf_op jit(solution)/shard_map/finish/pallas_call | solution.py:331
  (180 shorter events, 60.9 us)
Async XLA Ops:
  8.4 40.3 %collective-permute-start.44 = (bf16[1024,256]{1,0:T(8,128)(2,1)S(1)}, bf16[1024,256]{1,0:T(8,128)(2,1)S(1)}, u32[]{:S(2)}, u32[]{:S(2)}) collective-permute-start(bf16[1024,256]{1,0:T(8,128)(2,1)S(1)} %pick.3.refs_0_), channel_id=1, source_target_pairs={{0,1},{1,0},{2,3},{3,2},{4,5},{5,4},{6,7},{7,6},{8,9},{9,8},{10,11... | collective-permute-start | bytes 1572872 | tf_op jit(solution)/shard_map/ppermute | solution.py:387
  8.5 41.3 %collective-permute-start.28 = (bf16[1024,256]{1,0:T(8,128)(2,1)S(1)}, bf16[1024,256]{1,0:T(8,128)(2,1)S(1)}, u32[]{:S(2)}, u32[]{:S(2)}) collective-permute-start(bf16[1024,256]{1,0:T(8,128)(2,1)S(1)} %pick.3.refs_0_), channel_id=1, source_target_pairs={{0,4},{1,5},{4,8},{5,9},{8,12},{9,13},{12,14},{13,15},{14,10},{15,... | collective-permute-start | bytes 1572872 | tf_op jit(solution)/shard_map/ppermute | solution.py:384
  10.5 39.2 %collective-permute-start.33 = (bf16[1024,256]{1,0:T(8,128)(2,1)S(1)}, bf16[1024,256]{1,0:T(8,128)(2,1)S(1)}, u32[]{:S(2)}, u32[]{:S(2)}) collective-permute-start(bf16[1024,256]{1,0:T(8,128)(2,1)S(1)} %pick.3.refs_0_), channel_id=1, source_target_pairs={{0,2},{1,3},{4,0},{5,1},{8,4},{9,5},{12,8},{13,9},{14,12},{15,13},... | collective-permute-start | bytes 1572872 | tf_op jit(solution)/shard_map/ppermute | solution.py:384
  12.6 23.8 %collective-permute-start.24 = (bf16[96,768]{1,0:T(8,128)(2,1)S(1)}, bf16[96,768]{1,0:T(8,128)(2,1)S(1)}, u32[]{:S(2)}, u32[]{:S(2)}) collective-permute-start(bf16[96,768]{1,0:T(8,128)(2,1)S(1)} %pad_maximum_fusion.refs_3_.refs_5_.refs_0_), channel_id=1, source_target_pairs={{0,1},{1,0},{2,3},{3,2},{4,5},{5,4},{6,7},{7,6},{8,9},{9,8},{10,11... | collective-permute-start | bytes 442376 | tf_op jit(solution)/shard_map/ppermute | solution.py:387
  46.9 14.8 %collective-permute-start = (bf16[1024,256]{1,0:T(8,128)(2,1)S(1)}, bf16[1024,256]{1,0:T(8,128)(2,1)S(1)}, u32[]{:S(2)}, u32[]{:S(2)}) collective-permute-start(bf16[1024,256]{1,0:T(8,128)(2,1)S(1)} %pick.2.refs_0_), channel_id=1, source_target_pairs={{0,4},{1,5},{4,8},{5,9},{8,12},{9,13},{12,14},{13,15},{14,10},{15,... | collective-permute-start | bytes 1572872 | tf_op jit(solution)/shard_map/ppermute | solution.py:384
  49.5 14.7 %collective-permute-start.5 = (bf16[1024,256]{1,0:T(8,128)(2,1)S(1)}, bf16[1024,256]{1,0:T(8,128)(2,1)S(1)}, u32[]{:S(2)}, u32[]{:S(2)}) collective-permute-start(bf16[1024,256]{1,0:T(8,128)(2,1)S(1)} %pick.2.refs_0_), channel_id=1, source_target_pairs={{0,2},{1,3},{4,0},{5,1},{8,4},{9,5},{12,8},{13,9},{14,12},{15,13},... | collective-permute-start | bytes 1572872 | tf_op jit(solution)/shard_map/ppermute | solution.py:384
  49.8 14.4 %collective-permute-start.42 = (bf16[1024,256]{1,0:T(8,128)(2,1)S(1)}, bf16[1024,256]{1,0:T(8,128)(2,1)S(1)}, u32[]{:S(2)}, u32[]{:S(2)}) collective-permute-start(bf16[1024,256]{1,0:T(8,128)(2,1)S(1)} %collective-permute-done.28.refs_0_), channel_id=1, source_target_pairs={{0,1},{1,0},{2,3},{3,2},{4,5},{5,4},{6,7},{7,6},{8,9},{9,8},{10,11... | collective-permute-start | bytes 1572872 | tf_op jit(solution)/shard_map/ppermute | solution.py:387
  49.8 15.8 %collective-permute-start.43 = (bf16[1024,256]{1,0:T(8,128)(2,1)S(1)}, bf16[1024,256]{1,0:T(8,128)(2,1)S(1)}, u32[]{:S(2)}, u32[]{:S(2)}) collective-permute-start(bf16[1024,256]{1,0:T(8,128)(2,1)S(1)} %collective-permute-done.33.refs_1_), channel_id=1, source_target_pairs={{0,1},{1,0},{2,3},{3,2},{4,5},{5,4},{6,7},{7,6},{8,9},{9,8},{10,11... | collective-permute-start | bytes 1572872 | tf_op jit(solution)/shard_map/ppermute | solution.py:387
  51.1 21.8 %collective-permute-start.29 = (bf16[1024,256]{1,0:T(8,128)(2,1)S(1)}, bf16[1024,256]{1,0:T(8,128)(2,1)S(1)}, u32[]{:S(2)}, u32[]{:S(2)}) collective-permute-start(bf16[1024,256]{1,0:T(8,128)(2,1)S(1)} %collective-permute-done.28.refs_0_), channel_id=1, source_target_pairs={{0,4},{1,5},{4,8},{5,9},{8,12},{9,13},{12,14},{13,15},{14,10},{15,... | collective-permute-start | bytes 1572872 | tf_op jit(solution)/shard_map/ppermute | solution.py:384
  66.4 17.8 %collective-permute-start.1 = (bf16[1024,256]{1,0:T(8,128)(2,1)S(1)}, bf16[1024,256]{1,0:T(8,128)(2,1)S(1)}, u32[]{:S(2)}, u32[]{:S(2)}) collective-permute-start(bf16[1024,256]{1,0:T(8,128)(2,1)S(1)} %collective-permute-done.refs_0_), channel_id=1, source_target_pairs={{0,4},{1,5},{4,8},{5,9},{8,12},{9,13},{12,14},{13,15},{14,10},{15,... | collective-permute-start | bytes 1572872 | tf_op jit(solution)/shard_map/ppermute | solution.py:384
  77.6 17.8 %collective-permute-start.30 = (bf16[1024,256]{1,0:T(8,128)(2,1)S(1)}, bf16[1024,256]{1,0:T(8,128)(2,1)S(1)}, u32[]{:S(2)}, u32[]{:S(2)}) collective-permute-start(bf16[1024,256]{1,0:T(8,128)(2,1)S(1)} %collective-permute-done.29.refs_0_), channel_id=1, source_target_pairs={{0,4},{1,5},{4,8},{5,9},{8,12},{9,13},{12,14},{13,15},{14,10},{15,... | collective-permute-start | bytes 1572872 | tf_op jit(solution)/shard_map/ppermute | solution.py:384
  86.7 19.9 %collective-permute-start.2 = (bf16[1024,256]{1,0:T(8,128)(2,1)S(1)}, bf16[1024,256]{1,0:T(8,128)(2,1)S(1)}, u32[]{:S(2)}, u32[]{:S(2)}) collective-permute-start(bf16[1024,256]{1,0:T(8,128)(2,1)S(1)} %collective-permute-done.1.refs_0_), channel_id=1, source_target_pairs={{0,4},{1,5},{4,8},{5,9},{8,12},{9,13},{12,14},{13,15},{14,10},{15,... | collective-permute-start | bytes 1572872 | tf_op jit(solution)/shard_map/ppermute | solution.py:384
  88.3 20.0 %collective-permute-start.19 = (bf16[1024,256]{1,0:T(8,128)(2,1)S(1)}, bf16[1024,256]{1,0:T(8,128)(2,1)S(1)}, u32[]{:S(2)}, u32[]{:S(2)}) collective-permute-start(bf16[1024,256]{1,0:T(8,128)(2,1)S(1)} %collective-permute-done.1.refs_0_), channel_id=1, source_target_pairs={{0,1},{1,0},{2,3},{3,2},{4,5},{5,4},{6,7},{7,6},{8,9},{9,8},{10,11... | collective-permute-start | bytes 1572872 | tf_op jit(solution)/shard_map/ppermute | solution.py:387
  90.0 18.8 %collective-permute-start.20 = (bf16[1024,256]{1,0:T(8,128)(2,1)S(1)}, bf16[1024,256]{1,0:T(8,128)(2,1)S(1)}, u32[]{:S(2)}, u32[]{:S(2)}) collective-permute-start(bf16[1024,256]{1,0:T(8,128)(2,1)S(1)} %collective-permute-done.6.refs_1_), channel_id=1, source_target_pairs={{0,1},{1,0},{2,3},{3,2},{4,5},{5,4},{6,7},{7,6},{8,9},{9,8},{10,11... | collective-permute-start | bytes 1572872 | tf_op jit(solution)/shard_map/ppermute | solution.py:387
  95.4 14.2 %collective-permute-start.7 = (bf16[1024,256]{1,0:T(8,128)(2,1)S(1)}, bf16[1024,256]{1,0:T(8,128)(2,1)}, u32[]{:S(2)}, u32[]{:S(2)}) collective-permute-start(bf16[1024,256]{1,0:T(8,128)(2,1)S(1)} %collective-permute-done.6.refs_1_), channel_id=1, source_target_pairs={{0,2},{1,3},{4,0},{5,1},{8,4},{9,5},{12,8},{13,9},{14,12},{15,13},... | collective-permute-start | bytes 1572872 | tf_op jit(solution)/shard_map/ppermute | solution.py:384
  97.9 14.4 %collective-permute-start.31 = (bf16[512,256]{1,0:T(8,128)(2,1)S(1)}, bf16[512,256]{1,0:T(8,128)(2,1)}, u32[]{:S(2)}, u32[]{:S(2)}) collective-permute-start(bf16[512,256]{1,0:T(8,128)(2,1)S(1)} %slice.26), channel_id=1, source_target_pairs={{0,4},{1,5},{4,8},{5,9},{8,12},{9,13},{12,14},{13,15},{14,10},{15,... | collective-permute-start | bytes 786440 | tf_op jit(solution)/shard_map/ppermute | solution.py:384
  109.5 15.1 %collective-permute-start.38 = (bf16[1024,256]{1,0:T(8,128)(2,1)S(1)}, bf16[1024,256]{1,0:T(8,128)(2,1)S(1)}, u32[]{:S(2)}, u32[]{:S(2)}) collective-permute-start(bf16[1024,256]{1,0:T(8,128)(2,1)S(1)} %collective-permute-done.30.refs_0_), channel_id=1, source_target_pairs={{0,1},{1,0},{2,3},{3,2},{4,5},{5,4},{6,7},{7,6},{8,9},{9,8},{10,11... | collective-permute-start | bytes 1572872 | tf_op jit(solution)/shard_map/ppermute | solution.py:387
  109.5 16.4 %collective-permute-start.39 = (bf16[1024,256]{1,0:T(8,128)(2,1)S(1)}, bf16[1024,256]{1,0:T(8,128)(2,1)S(1)}, u32[]{:S(2)}, u32[]{:S(2)}) collective-permute-start(bf16[1024,256]{1,0:T(8,128)(2,1)S(1)} %collective-permute-done.35.refs_1_), channel_id=1, source_target_pairs={{0,1},{1,0},{2,3},{3,2},{4,5},{5,4},{6,7},{7,6},{8,9},{9,8},{10,11... | collective-permute-start | bytes 1572872 | tf_op jit(solution)/shard_map/ppermute | solution.py:387
  112.3 14.4 %collective-permute-start.10 = (bf16[1024,256]{1,0:T(8,128)(2,1)S(1)}, bf16[1024,256]{1,0:T(8,128)(2,1)S(1)}, u32[]{:S(2)}, u32[]{:S(2)}) collective-permute-start(bf16[1024,256]{1,0:T(8,128)(2,1)S(1)} %collective-permute-done.2.refs_0_), channel_id=1, source_target_pairs={{0,1},{1,0},{2,3},{3,2},{4,5},{5,4},{6,7},{7,6},{8,9},{9,8},{10,11... | collective-permute-start | bytes 1572872 | tf_op jit(solution)/shard_map/ppermute | solution.py:387
  113.8 45.8 %collective-permute-start.11 = (bf16[1024,256]{1,0:T(8,128)(2,1)}, bf16[1024,256]{1,0:T(8,128)(2,1)}, u32[]{:S(2)}, u32[]{:S(2)}) collective-permute-start(bf16[1024,256]{1,0:T(8,128)(2,1)} %collective-permute-done.7.refs_1_), channel_id=1, source_target_pairs={{0,1},{1,0},{2,3},{3,2},{4,5},{5,4},{6,7},{7,6},{8,9},{9,8},{10,11... | collective-permute-start | bytes 1572872 | tf_op jit(solution)/shard_map/ppermute | solution.py:387
  124.7 38.3 %collective-permute-start.32 = (bf16[512,256]{1,0:T(8,128)(2,1)}, bf16[512,256]{1,0:T(8,128)(2,1)}, u32[]{:S(2)}, u32[]{:S(2)}) collective-permute-start(bf16[512,256]{1,0:T(8,128)(2,1)} %collective-permute-done.31.refs_0_), channel_id=1, source_target_pairs={{0,1},{1,0},{2,3},{3,2},{4,5},{5,4},{6,7},{7,6},{8,9},{9,8},{10,11... | collective-permute-start | bytes 786440 | tf_op jit(solution)/shard_map/ppermute | solution.py:387
  125.5 37.5 %collective-permute-start.37 = (bf16[512,256]{1,0:T(8,128)(2,1)}, bf16[512,256]{1,0:T(8,128)(2,1)}, u32[]{:S(2)}, u32[]{:S(2)}) collective-permute-start(bf16[512,256]{1,0:T(8,128)(2,1)} %collective-permute-done.36.refs_2_), channel_id=1, source_target_pairs={{0,1},{1,0},{2,3},{3,2},{4,5},{5,4},{6,7},{7,6},{8,9},{9,8},{10,11... | collective-permute-start | bytes 786440 | tf_op jit(solution)/shard_map/ppermute | solution.py:387
  126.8 40.6 %collective-permute-start.4 = (bf16[512,256]{1,0:T(8,128)(2,1)}, bf16[512,256]{1,0:T(8,128)(2,1)}, u32[]{:S(2)}, u32[]{:S(2)}) collective-permute-start(bf16[512,256]{1,0:T(8,128)(2,1)} %collective-permute-done.3.refs_0_), channel_id=1, source_target_pairs={{0,1},{1,0},{2,3},{3,2},{4,5},{5,4},{6,7},{7,6},{8,9},{9,8},{10,11... | collective-permute-start | bytes 786440 | tf_op jit(solution)/shard_map/ppermute | solution.py:387
  127.6 39.8 %collective-permute-start.9 = (bf16[512,256]{1,0:T(8,128)(2,1)}, bf16[512,256]{1,0:T(8,128)(2,1)}, u32[]{:S(2)}, u32[]{:S(2)}) collective-permute-start(bf16[512,256]{1,0:T(8,128)(2,1)} %collective-permute-done.8.refs_2_), channel_id=1, source_target_pairs={{0,1},{1,0},{2,3},{3,2},{4,5},{5,4},{6,7},{7,6},{8,9},{9,8},{10,11... | collective-permute-start | bytes 786440 | tf_op jit(solution)/shard_map/ppermute | solution.py:387
  (66 other events, 436.6 us)

commit v3 on v2

--- a/solution.py
+++ b/solution.py
@@ -12,6 +12,7 @@
 epsilon = 1e-06
 LANES = 128
 PARTS = 1
+FINISH_ROWS = 256
 
 
 def dot32(a, b):
@@ -282,13 +283,18 @@
     p_ref, l_ref, q_ref, e_ref, mine_ref, theirs_ref, d_ref, norm_ref = refs[2 * sides : 2 * sides + 8]
     out_ref, o_ref, sems = refs[-3:]
     genes = o_ref.shape[1]
-    tile = refs[0].shape[0]
+    whole = refs[0].shape[0]
+    tile = min(whole, FINISH_ROWS)
+    cuts = whole // tile
     mine, theirs = mine_ref[...], theirs_ref[...]
     gene_scale = scale * lax.rsqrt(norm_ref[...] + epsilon)
     copies = []
-    for k in range(sides):
-        here = slice(starts[k], starts[k] + tile)
-        x, e = both_halves(refs[2 * k : 2 * k + 2], e_ref, at)
+    for k in range(sides * cuts):
+        side, cut = divmod(k, cuts)
+        start = starts[side] + cut * tile
+        here = slice(start, start + tile)
+        pieces = [r.at[cut * tile : (cut + 1) * tile, :] for r in refs[2 * side : 2 * side + 2]]
+        x, e = both_halves(pieces, e_ref, at)
         l, q = loads_and_squares(x, mine, theirs, l_ref[here, :], q_ref[here, :])
         blank = -l.shape[1] % LANES
         if blank:
@@ -305,7 +311,7 @@
         copies.append(
             pltpu.make_async_copy(
                 o_ref.at[pl.ds(k * tile, tile), :],
-                out_ref.at[pl.ds(first + starts[k], tile), :],
+                out_ref.at[pl.ds(first + start, tile), :],
                 sems.at[k],
             )
         )
@@ -343,7 +349,7 @@
         out_shape=jax.ShapeDtypeStruct((blocks * width, genes), jnp.float32),
         scratch_shapes=[
             pltpu.VMEM((sides * tile, genes), jnp.float32),
-            pltpu.SemaphoreType.DMA((sides,)),
+            pltpu.SemaphoreType.DMA((sides * -(-tile // FINISH_ROWS),)),
         ],
         input_output_aliases=aliases,
         compiler_params=limit(20),

time: 172 us -> 173 us (level)
  no operation moved by 1% of the time
where the time goes in v3:
time: 173 us; the launch traced here: 172 us
  waiting for transfers between devices  63.8 us (37%)
  Pallas kernels  52.5 us (30%)
  starting transfers between devices  37.1 us (21%)
  local copies, waits for them, and re-layouts  18.2 us (11%)
    ppermute x23, waiting for transfers between devices, shift(): return lax.ppermute(x, 'samp', pairs)  63.1 us
    ppermute x23, starting transfers between devices, shift(): return lax.ppermute(x, 'samp', pairs)  32.3 us
    unnamed x92, local copies, waits for them, and re-layouts  16.4 us
    pallas_call x8, Pallas kernels, fold(): pl.pallas_call(functools.partial(fold_kernel, pieces=pieces, at=at, fresh...  15.8 us
    pallas_call x2, Pallas kernels, finish(): pl.pallas_call(functools.partial(finish_kernel, sides=sides, at=at, scale...  9.34 us
    pallas_call x1, Pallas kernels, solve(): pl.pallas_call(solve_kernel, grid=(1,), in_specs=[pl.BlockSpec(a.shape, l...  9.3 us
    pallas_call x2, Pallas kernels, pick(): pl.pallas_call(pick_kernel, grid_spec=pltpu.PrefetchScalarGridSpec(num_sc...  9.06 us
    pallas_call x1, Pallas kernels, match(): pl.pallas_call(functools.partial(match_kernel, chips=chips), grid_spec=pl...  9.03 us
  transfers between devices with their start and end apart: 45, of which 15 were waited for; matrix products, arithmetic and copies ran while one was open for 1% of the time, Pallas kernels for 28%

profile of v3, /device:TPU:0, one launch (start us, length us, event | category | flops | bytes accessed | tf_op | source)
XLA Modules:
  0.0 172.5 jit_solution(6039941913256995611)
XLA Ops:
  0.0 3.1 %collective-permute-start.12 = (bf16[96,256]{1,0:T(8,128)(2,1)}, bf16[96,256]{1,0:T(8,128)(2,1)S(1)}, u32[]{:S(2)}, u32[]{:S(2)}) collective-permute-start(bf16[96,256]{1,0:T(8,128)(2,1)} %bitcast.6), channel_id=1, source_target_pairs={{0,4},{1,5},{4,8},{5,9},{8,12},{9,13},{12,14},{13,15},{14,10},{15,... | collective-permute-start | bytes 147464 | tf_op jit(solution)/shard_map/ppermute | solution.py:390
  3.9 4.5 %pick.3.refs_0_ = bf16[1024,256]{1,0:T(8,128)(2,1)S(1)} custom-call(s32[1024]{0:T(1024)S(1)} %bitcast.5, bf16[256,8192]{1,0:T(8,128)(2,1)} %x_hbm.3), custom_call_target="tpu_custom_call" | custom-call | tf_op jit(solution)/shard_map/pick/pallas_call | solution.py:73
  8.5 2.1 %collective-permute-start.28 = (bf16[1024,256]{1,0:T(8,128)(2,1)S(1)}, bf16[1024,256]{1,0:T(8,128)(2,1)S(1)}, u32[]{:S(2)}, u32[]{:S(2)}) collective-permute-start(bf16[1024,256]{1,0:T(8,128)(2,1)S(1)} %pick.3.refs_0_), channel_id=1, source_target_pairs={{0,4},{1,5},{4,8},{5,9},{8,12},{9,13},{12,14},{13,15},{14,10},{15,... | collective-permute-start | bytes 1572872 | tf_op jit(solution)/shard_map/ppermute | solution.py:390
  12.7 11.4 %collective-permute-done.13 = bf16[96,256]{1,0:T(8,128)(2,1)S(1)} collective-permute-done((bf16[96,256]{1,0:T(8,128)(2,1)S(1)}, bf16[96,256]{1,0:T(8,128)(2,1)S(1)}, u32[]{:S(2)}, u32[]{:S(2)}) %collective-permute-start.13) | collective-permute-done | bytes 49184 | tf_op jit(solution)/shard_map/ppermute | solution.py:390
  25.8 2.3 %collective-permute-done.16 = bf16[96,256]{1,0:T(8,128)(2,1)S(1)} collective-permute-done((bf16[96,256]{1,0:T(8,128)(2,1)S(1)}, bf16[96,256]{1,0:T(8,128)(2,1)S(1)}, u32[]{:S(2)}, u32[]{:S(2)}) %collective-permute-start.16) | collective-permute-done | bytes 49184 | tf_op jit(solution)/shard_map/ppermute | solution.py:390
  30.0 2.3 %collective-permute-done.14 = bf16[96,256]{1,0:T(8,128)(2,1)S(1)} collective-permute-done((bf16[96,256]{1,0:T(8,128)(2,1)S(1)}, bf16[96,256]{1,0:T(8,128)(2,1)S(1)}, u32[]{:S(2)}, u32[]{:S(2)}) %collective-permute-start.14) | collective-permute-done | bytes 49184 | tf_op jit(solution)/shard_map/ppermute | solution.py:390
  34.0 2.3 %collective-permute-done.17 = bf16[96,256]{1,0:T(8,128)(2,1)S(1)} collective-permute-done((bf16[96,256]{1,0:T(8,128)(2,1)S(1)}, bf16[96,256]{1,0:T(8,128)(2,1)S(1)}, u32[]{:S(2)}, u32[]{:S(2)}) %collective-permute-start.17) | collective-permute-done | bytes 49184 | tf_op jit(solution)/shard_map/ppermute | solution.py:390
  39.4 2.3 %collective-permute-done.26.refs_3_.refs_8_ = bf16[96,256]{1,0:T(8,128)(2,1)S(1)} collective-permute-done((bf16[96,256]{1,0:T(8,128)(2,1)S(1)}, bf16[96,256]{1,0:T(8,128)(2,1)S(1)}, u32[]{:S(2)}, u32[]{:S(2)}) %collective-permute-start.26) | collective-permute-done | bytes 49184 | tf_op jit(solution)/shard_map/ppermute | solution.py:390
  41.7 4.5 %pick.2.refs_0_ = bf16[1024,256]{1,0:T(8,128)(2,1)S(1)} custom-call(s32[1024]{0:T(1024)S(1)} %bitcast.4, bf16[256,8192]{1,0:T(8,128)(2,1)} %x_hbm.3), custom_call_target="tpu_custom_call" | custom-call | tf_op jit(solution)/shard_map/pick/pallas_call | solution.py:73
  53.7 8.0 %collective-permute-done.refs_0_ = bf16[1024,256]{1,0:T(8,128)(2,1)S(1)} collective-permute-done((bf16[1024,256]{1,0:T(8,128)(2,1)S(1)}, bf16[1024,256]{1,0:T(8,128)(2,1)S(1)}, u32[]{:S(2)}, u32[]{:S(2)}) %collective-permute-start) | collective-permute-done | bytes 524320 | tf_op jit(solution)/shard_map/ppermute | solution.py:390
  68.1 4.8 %collective-permute-done.29.refs_0_ = bf16[1024,256]{1,0:T(8,128)(2,1)S(1)} collective-permute-done((bf16[1024,256]{1,0:T(8,128)(2,1)S(1)}, bf16[1024,256]{1,0:T(8,128)(2,1)S(1)}, u32[]{:S(2)}, u32[]{:S(2)}) %collective-permute-start.29) | collective-permute-done | bytes 524320 | tf_op jit(solution)/shard_map/ppermute | solution.py:390
  79.2 4.9 %collective-permute-done.1.refs_0_ = bf16[1024,256]{1,0:T(8,128)(2,1)S(1)} collective-permute-done((bf16[1024,256]{1,0:T(8,128)(2,1)S(1)}, bf16[1024,256]{1,0:T(8,128)(2,1)S(1)}, u32[]{:S(2)}, u32[]{:S(2)}) %collective-permute-start.1) | collective-permute-done | bytes 524320 | tf_op jit(solution)/shard_map/ppermute | solution.py:390
  90.5 4.9 %collective-permute-done.30.refs_0_ = bf16[1024,256]{1,0:T(8,128)(2,1)S(1)} collective-permute-done((bf16[1024,256]{1,0:T(8,128)(2,1)S(1)}, bf16[1024,256]{1,0:T(8,128)(2,1)S(1)}, u32[]{:S(2)}, u32[]{:S(2)}) %collective-permute-start.30) | collective-permute-done | bytes 524320 | tf_op jit(solution)/shard_map/ppermute | solution.py:390
  98.8 7.8 %collective-permute-done.2.refs_0_ = bf16[1024,256]{1,0:T(8,128)(2,1)S(1)} collective-permute-done((bf16[1024,256]{1,0:T(8,128)(2,1)S(1)}, bf16[1024,256]{1,0:T(8,128)(2,1)S(1)}, u32[]{:S(2)}, u32[]{:S(2)}) %collective-permute-start.2) | collective-permute-done | bytes 524320 | tf_op jit(solution)/shard_map/ppermute | solution.py:390
  110.1 2.3 %collective-permute-done.31.refs_0_ = bf16[512,256]{1,0:T(8,128)(2,1)} collective-permute-done((bf16[512,256]{1,0:T(8,128)(2,1)S(1)}, bf16[512,256]{1,0:T(8,128)(2,1)}, u32[]{:S(2)}, u32[]{:S(2)}) %collective-permute-start.31) | collective-permute-done | bytes 262176 | tf_op jit(solution)/shard_map/ppermute | solution.py:390
  114.8 2.3 %collective-permute-done.3.refs_0_ = bf16[512,256]{1,0:T(8,128)(2,1)} collective-permute-done((bf16[512,256]{1,0:T(8,128)(2,1)S(1)}, bf16[512,256]{1,0:T(8,128)(2,1)}, u32[]{:S(2)}, u32[]{:S(2)}) %collective-permute-start.3) | collective-permute-done | bytes 262176 | tf_op jit(solution)/shard_map/ppermute | solution.py:390
  118.8 5.8 %collective-permute-done.8.refs_2_ = bf16[512,256]{1,0:T(8,128)(2,1)} collective-permute-done((bf16[512,256]{1,0:T(8,128)(2,1)S(1)}, bf16[512,256]{1,0:T(8,128)(2,1)}, u32[]{:S(2)}, u32[]{:S(2)}) %collective-permute-start.8) | collective-permute-done | bytes 262176 | tf_op jit(solution)/shard_map/ppermute | solution.py:390
  128.1 9.0 %match.1 = (bf16[4096,512]{1,0:T(8,128)(2,1)S(1)}, f32[1,512]{1,0:T(1,128)S(1)}) custom-call(s32[4096]{0:T(1024)S(1)} %copy-done.42, s32[24]{0:T(128)S(1)} %copy-done.43, s32[1]{0:T(128)} %bitcast.1.me_ref, bf16[4096,512]{1,0:T(8,128)(2,1)} %e_hbm.1), custom_call_target="tpu_custom_call" | custom-call | tf_op jit(solution)/shard_map/match/pallas_call | solution.py:136
  137.1 9.3 %solve.1.refs_10_ = bf16[768,640]{1,0:T(8,128)(2,1)S(1)} custom-call(bf16[96,768]{1,0:T(8,128)(2,1)S(1)} %pad_maximum_fusion.refs_3_.refs_5_.refs_0_, bf16[96,512]{1,0:T(8,128)(2,1)S(1)} %constant_dynamic-update-slice_fusion.2.refs_5_.refs_1_, bf16[96,512]{1,0:T(8,128)(2,1)S(1)} %constant_dynamic-update-slice_fusion.refs_5_.refs_2_, ...), custom_call_target="tpu_custom_call" | custom-call | tf_op jit(solution)/shard_map/solve/pallas_call | solution.py:271
  149.2 2.0 %fold.13 = (f32[1024,512]{1,0:T(8,128)S(1)}, f32[1024,96]{1,0:T(8,128)S(1)}, f32[1024,128]{1,0:T(8,128)S(1)}) custom-call(bf16[1024,256]{1,0:T(8,128)(2,1)S(1)} %copy-done.1, bf16[1024,256]{1,0:T(8,128)(2,1)S(1)} %copy-done.3, bf16[1024,256]{1,0:T(8,128)(2,1)S(1)} %copy-done.13, ...), custom_call_target="tpu_custom_call", output_to_operand_aliasing={{0}: (7, {}), {1}: (8, {}), {2}: (9, {})} | custom-call | tf_op jit(solution)/shard_map/fold/pallas_call | solution.py:212
  151.3 2.0 %fold.9 = (f32[1024,512]{1,0:T(8,128)S(1)}, f32[1024,96]{1,0:T(8,128)S(1)}, f32[1024,128]{1,0:T(8,128)S(1)}) custom-call(bf16[1024,256]{1,0:T(8,128)(2,1)S(1)} %copy-done.5, bf16[1024,256]{1,0:T(8,128)(2,1)S(1)} %copy-done.7, bf16[1024,256]{1,0:T(8,128)(2,1)S(1)} %copy-done.21, ...), custom_call_target="tpu_custom_call", output_to_operand_aliasing={{0}: (7, {}), {1}: (8, {}), {2}: (9, {})} | custom-call | tf_op jit(solution)/shard_map/fold/pallas_call | solution.py:212
  159.6 3.3 %fold.11 = (f32[1024,512]{1,0:T(8,128)S(1)}, f32[1024,96]{1,0:T(8,128)S(1)}, f32[1024,128]{1,0:T(8,128)S(1)}) custom-call(bf16[1024,256]{1,0:T(8,128)(2,1)S(1)} %collective-permute-done.2.refs_0_, bf16[1024,256]{1,0:T(8,128)(2,1)} %collective-permute-done.7.refs_1_, ...), custom_call_target="tpu_custom_call", output_to_operand_aliasing={{0}: (7, {}), {1}: (8, {}), {2}: (9, {})} | custom-call | tf_op jit(solution)/shard_map/fold/pallas_call | solution.py:212
  162.9 4.7 %finish.2.refs_12_ = f32[2048,512]{1,0:T(8,128)} custom-call(bf16[512,256]{1,0:T(8,128)(2,1)} %collective-permute-done.31.refs_0_, bf16[512,256]{1,0:T(8,128)(2,1)} %collective-permute-done.32.refs_1_, bf16[512,256]{1,0:T(8,128)(2,1)} %collective-permute-done.36.refs_2_, bf16[512,256]{1,0:T(8,128)(2,1)} %collective-permute-done.37.refs_3_, ...), custom_call_target="tpu_custom_call" | custom-call | tf_op jit(solution)/shard_map/finish/pallas_call | solution.py:337
  167.6 4.7 %finish.3 = f32[2048,512]{1,0:T(8,128)} custom-call(bf16[512,256]{1,0:T(8,128)(2,1)} %collective-permute-done.3.refs_0_, bf16[512,256]{1,0:T(8,128)(2,1)} %collective-permute-done.4.refs_1_, bf16[512,256]{1,0:T(8,128)(2,1)} %collective-permute-done.8.refs_2_, bf16[512,256]{1,0:T(8,128)(2,1)} %collective-permute-done.9.refs_3_, ...), custom_call_target="tpu_custom_call", output_to_operand_aliasing={{}: (12, {})} | custom-call | tf_op jit(solution)/shard_map/finish/pallas_call | solution.py:337
  (180 shorter events, 60.9 us)
Async XLA Ops:
  8.4 40.3 %collective-permute-start.44 = (bf16[1024,256]{1,0:T(8,128)(2,1)S(1)}, bf16[1024,256]{1,0:T(8,128)(2,1)S(1)}, u32[]{:S(2)}, u32[]{:S(2)}) collective-permute-start(bf16[1024,256]{1,0:T(8,128)(2,1)S(1)} %pick.3.refs_0_), channel_id=1, source_target_pairs={{0,1},{1,0},{2,3},{3,2},{4,5},{5,4},{6,7},{7,6},{8,9},{9,8},{10,11... | collective-permute-start | bytes 1572872 | tf_op jit(solution)/shard_map/ppermute | solution.py:393
  8.5 41.3 %collective-permute-start.28 = (bf16[1024,256]{1,0:T(8,128)(2,1)S(1)}, bf16[1024,256]{1,0:T(8,128)(2,1)S(1)}, u32[]{:S(2)}, u32[]{:S(2)}) collective-permute-start(bf16[1024,256]{1,0:T(8,128)(2,1)S(1)} %pick.3.refs_0_), channel_id=1, source_target_pairs={{0,4},{1,5},{4,8},{5,9},{8,12},{9,13},{12,14},{13,15},{14,10},{15,... | collective-permute-start | bytes 1572872 | tf_op jit(solution)/shard_map/ppermute | solution.py:390
  10.5 39.2 %collective-permute-start.33 = (bf16[1024,256]{1,0:T(8,128)(2,1)S(1)}, bf16[1024,256]{1,0:T(8,128)(2,1)S(1)}, u32[]{:S(2)}, u32[]{:S(2)}) collective-permute-start(bf16[1024,256]{1,0:T(8,128)(2,1)S(1)} %pick.3.refs_0_), channel_id=1, source_target_pairs={{0,2},{1,3},{4,0},{5,1},{8,4},{9,5},{12,8},{13,9},{14,12},{15,13},... | collective-permute-start | bytes 1572872 | tf_op jit(solution)/shard_map/ppermute | solution.py:390
  12.6 23.8 %collective-permute-start.24 = (bf16[96,768]{1,0:T(8,128)(2,1)S(1)}, bf16[96,768]{1,0:T(8,128)(2,1)S(1)}, u32[]{:S(2)}, u32[]{:S(2)}) collective-permute-start(bf16[96,768]{1,0:T(8,128)(2,1)S(1)} %pad_maximum_fusion.refs_3_.refs_5_.refs_0_), channel_id=1, source_target_pairs={{0,1},{1,0},{2,3},{3,2},{4,5},{5,4},{6,7},{7,6},{8,9},{9,8},{10,11... | collective-permute-start | bytes 442376 | tf_op jit(solution)/shard_map/ppermute | solution.py:393
  46.9 14.8 %collective-permute-start = (bf16[1024,256]{1,0:T(8,128)(2,1)S(1)}, bf16[1024,256]{1,0:T(8,128)(2,1)S(1)}, u32[]{:S(2)}, u32[]{:S(2)}) collective-permute-start(bf16[1024,256]{1,0:T(8,128)(2,1)S(1)} %pick.2.refs_0_), channel_id=1, source_target_pairs={{0,4},{1,5},{4,8},{5,9},{8,12},{9,13},{12,14},{13,15},{14,10},{15,... | collective-permute-start | bytes 1572872 | tf_op jit(solution)/shard_map/ppermute | solution.py:390
  49.5 14.7 %collective-permute-start.5 = (bf16[1024,256]{1,0:T(8,128)(2,1)S(1)}, bf16[1024,256]{1,0:T(8,128)(2,1)S(1)}, u32[]{:S(2)}, u32[]{:S(2)}) collective-permute-start(bf16[1024,256]{1,0:T(8,128)(2,1)S(1)} %pick.2.refs_0_), channel_id=1, source_target_pairs={{0,2},{1,3},{4,0},{5,1},{8,4},{9,5},{12,8},{13,9},{14,12},{15,13},... | collective-permute-start | bytes 1572872 | tf_op jit(solution)/shard_map/ppermute | solution.py:390
  49.8 14.4 %collective-permute-start.42 = (bf16[1024,256]{1,0:T(8,128)(2,1)S(1)}, bf16[1024,256]{1,0:T(8,128)(2,1)S(1)}, u32[]{:S(2)}, u32[]{:S(2)}) collective-permute-start(bf16[1024,256]{1,0:T(8,128)(2,1)S(1)} %collective-permute-done.28.refs_0_), channel_id=1, source_target_pairs={{0,1},{1,0},{2,3},{3,2},{4,5},{5,4},{6,7},{7,6},{8,9},{9,8},{10,11... | collective-permute-start | bytes 1572872 | tf_op jit(solution)/shard_map/ppermute | solution.py:393
  49.8 15.8 %collective-permute-start.43 = (bf16[1024,256]{1,0:T(8,128)(2,1)S(1)}, bf16[1024,256]{1,0:T(8,128)(2,1)S(1)}, u32[]{:S(2)}, u32[]{:S(2)}) collective-permute-start(bf16[1024,256]{1,0:T(8,128)(2,1)S(1)} %collective-permute-done.33.refs_1_), channel_id=1, source_target_pairs={{0,1},{1,0},{2,3},{3,2},{4,5},{5,4},{6,7},{7,6},{8,9},{9,8},{10,11... | collective-permute-start | bytes 1572872 | tf_op jit(solution)/shard_map/ppermute | solution.py:393
  51.1 21.8 %collective-permute-start.29 = (bf16[1024,256]{1,0:T(8,128)(2,1)S(1)}, bf16[1024,256]{1,0:T(8,128)(2,1)S(1)}, u32[]{:S(2)}, u32[]{:S(2)}) collective-permute-start(bf16[1024,256]{1,0:T(8,128)(2,1)S(1)} %collective-permute-done.28.refs_0_), channel_id=1, source_target_pairs={{0,4},{1,5},{4,8},{5,9},{8,12},{9,13},{12,14},{13,15},{14,10},{15,... | collective-permute-start | bytes 1572872 | tf_op jit(solution)/shard_map/ppermute | solution.py:390
  66.4 17.8 %collective-permute-start.1 = (bf16[1024,256]{1,0:T(8,128)(2,1)S(1)}, bf16[1024,256]{1,0:T(8,128)(2,1)S(1)}, u32[]{:S(2)}, u32[]{:S(2)}) collective-permute-start(bf16[1024,256]{1,0:T(8,128)(2,1)S(1)} %collective-permute-done.refs_0_), channel_id=1, source_target_pairs={{0,4},{1,5},{4,8},{5,9},{8,12},{9,13},{12,14},{13,15},{14,10},{15,... | collective-permute-start | bytes 1572872 | tf_op jit(solution)/shard_map/ppermute | solution.py:390
  77.6 17.8 %collective-permute-start.30 = (bf16[1024,256]{1,0:T(8,128)(2,1)S(1)}, bf16[1024,256]{1,0:T(8,128)(2,1)S(1)}, u32[]{:S(2)}, u32[]{:S(2)}) collective-permute-start(bf16[1024,256]{1,0:T(8,128)(2,1)S(1)} %collective-permute-done.29.refs_0_), channel_id=1, source_target_pairs={{0,4},{1,5},{4,8},{5,9},{8,12},{9,13},{12,14},{13,15},{14,10},{15,... | collective-permute-start | bytes 1572872 | tf_op jit(solution)/shard_map/ppermute | solution.py:390
  86.7 19.9 %collective-permute-start.2 = (bf16[1024,256]{1,0:T(8,128)(2,1)S(1)}, bf16[1024,256]{1,0:T(8,128)(2,1)S(1)}, u32[]{:S(2)}, u32[]{:S(2)}) collective-permute-start(bf16[1024,256]{1,0:T(8,128)(2,1)S(1)} %collective-permute-done.1.refs_0_), channel_id=1, source_target_pairs={{0,4},{1,5},{4,8},{5,9},{8,12},{9,13},{12,14},{13,15},{14,10},{15,... | collective-permute-start | bytes 1572872 | tf_op jit(solution)/shard_map/ppermute | solution.py:390
  88.3 20.0 %collective-permute-start.19 = (bf16[1024,256]{1,0:T(8,128)(2,1)S(1)}, bf16[1024,256]{1,0:T(8,128)(2,1)S(1)}, u32[]{:S(2)}, u32[]{:S(2)}) collective-permute-start(bf16[1024,256]{1,0:T(8,128)(2,1)S(1)} %collective-permute-done.1.refs_0_), channel_id=1, source_target_pairs={{0,1},{1,0},{2,3},{3,2},{4,5},{5,4},{6,7},{7,6},{8,9},{9,8},{10,11... | collective-permute-start | bytes 1572872 | tf_op jit(solution)/shard_map/ppermute | solution.py:393
  90.0 18.8 %collective-permute-start.20 = (bf16[1024,256]{1,0:T(8,128)(2,1)S(1)}, bf16[1024,256]{1,0:T(8,128)(2,1)S(1)}, u32[]{:S(2)}, u32[]{:S(2)}) collective-permute-start(bf16[1024,256]{1,0:T(8,128)(2,1)S(1)} %collective-permute-done.6.refs_1_), channel_id=1, source_target_pairs={{0,1},{1,0},{2,3},{3,2},{4,5},{5,4},{6,7},{7,6},{8,9},{9,8},{10,11... | collective-permute-start | bytes 1572872 | tf_op jit(solution)/shard_map/ppermute | solution.py:393
  95.4 14.2 %collective-permute-start.7 = (bf16[1024,256]{1,0:T(8,128)(2,1)S(1)}, bf16[1024,256]{1,0:T(8,128)(2,1)}, u32[]{:S(2)}, u32[]{:S(2)}) collective-permute-start(bf16[1024,256]{1,0:T(8,128)(2,1)S(1)} %collective-permute-done.6.refs_1_), channel_id=1, source_target_pairs={{0,2},{1,3},{4,0},{5,1},{8,4},{9,5},{12,8},{13,9},{14,12},{15,13},... | collective-permute-start | bytes 1572872 | tf_op jit(solution)/shard_map/ppermute | solution.py:390
  97.9 14.4 %collective-permute-start.31 = (bf16[512,256]{1,0:T(8,128)(2,1)S(1)}, bf16[512,256]{1,0:T(8,128)(2,1)}, u32[]{:S(2)}, u32[]{:S(2)}) collective-permute-start(bf16[512,256]{1,0:T(8,128)(2,1)S(1)} %slice.26), channel_id=1, source_target_pairs={{0,4},{1,5},{4,8},{5,9},{8,12},{9,13},{12,14},{13,15},{14,10},{15,... | collective-permute-start | bytes 786440 | tf_op jit(solution)/shard_map/ppermute | solution.py:390
  109.5 15.1 %collective-permute-start.38 = (bf16[1024,256]{1,0:T(8,128)(2,1)S(1)}, bf16[1024,256]{1,0:T(8,128)(2,1)S(1)}, u32[]{:S(2)}, u32[]{:S(2)}) collective-permute-start(bf16[1024,256]{1,0:T(8,128)(2,1)S(1)} %collective-permute-done.30.refs_0_), channel_id=1, source_target_pairs={{0,1},{1,0},{2,3},{3,2},{4,5},{5,4},{6,7},{7,6},{8,9},{9,8},{10,11... | collective-permute-start | bytes 1572872 | tf_op jit(solution)/shard_map/ppermute | solution.py:393
  109.5 16.4 %collective-permute-start.39 = (bf16[1024,256]{1,0:T(8,128)(2,1)S(1)}, bf16[1024,256]{1,0:T(8,128)(2,1)S(1)}, u32[]{:S(2)}, u32[]{:S(2)}) collective-permute-start(bf16[1024,256]{1,0:T(8,128)(2,1)S(1)} %collective-permute-done.35.refs_1_), channel_id=1, source_target_pairs={{0,1},{1,0},{2,3},{3,2},{4,5},{5,4},{6,7},{7,6},{8,9},{9,8},{10,11... | collective-permute-start | bytes 1572872 | tf_op jit(solution)/shard_map/ppermute | solution.py:393
  112.3 14.4 %collective-permute-start.10 = (bf16[1024,256]{1,0:T(8,128)(2,1)S(1)}, bf16[1024,256]{1,0:T(8,128)(2,1)S(1)}, u32[]{:S(2)}, u32[]{:S(2)}) collective-permute-start(bf16[1024,256]{1,0:T(8,128)(2,1)S(1)} %collective-permute-done.2.refs_0_), channel_id=1, source_target_pairs={{0,1},{1,0},{2,3},{3,2},{4,5},{5,4},{6,7},{7,6},{8,9},{9,8},{10,11... | collective-permute-start | bytes 1572872 | tf_op jit(solution)/shard_map/ppermute | solution.py:393
  113.8 45.8 %collective-permute-start.11 = (bf16[1024,256]{1,0:T(8,128)(2,1)}, bf16[1024,256]{1,0:T(8,128)(2,1)}, u32[]{:S(2)}, u32[]{:S(2)}) collective-permute-start(bf16[1024,256]{1,0:T(8,128)(2,1)} %collective-permute-done.7.refs_1_), channel_id=1, source_target_pairs={{0,1},{1,0},{2,3},{3,2},{4,5},{5,4},{6,7},{7,6},{8,9},{9,8},{10,11... | collective-permute-start | bytes 1572872 | tf_op jit(solution)/shard_map/ppermute | solution.py:393
  124.7 38.3 %collective-permute-start.32 = (bf16[512,256]{1,0:T(8,128)(2,1)}, bf16[512,256]{1,0:T(8,128)(2,1)}, u32[]{:S(2)}, u32[]{:S(2)}) collective-permute-start(bf16[512,256]{1,0:T(8,128)(2,1)} %collective-permute-done.31.refs_0_), channel_id=1, source_target_pairs={{0,1},{1,0},{2,3},{3,2},{4,5},{5,4},{6,7},{7,6},{8,9},{9,8},{10,11... | collective-permute-start | bytes 786440 | tf_op jit(solution)/shard_map/ppermute | solution.py:393
  125.5 37.5 %collective-permute-start.37 = (bf16[512,256]{1,0:T(8,128)(2,1)}, bf16[512,256]{1,0:T(8,128)(2,1)}, u32[]{:S(2)}, u32[]{:S(2)}) collective-permute-start(bf16[512,256]{1,0:T(8,128)(2,1)} %collective-permute-done.36.refs_2_), channel_id=1, source_target_pairs={{0,1},{1,0},{2,3},{3,2},{4,5},{5,4},{6,7},{7,6},{8,9},{9,8},{10,11... | collective-permute-start | bytes 786440 | tf_op jit(solution)/shard_map/ppermute | solution.py:393
  126.8 40.8 %collective-permute-start.4 = (bf16[512,256]{1,0:T(8,128)(2,1)}, bf16[512,256]{1,0:T(8,128)(2,1)}, u32[]{:S(2)}, u32[]{:S(2)}) collective-permute-start(bf16[512,256]{1,0:T(8,128)(2,1)} %collective-permute-done.3.refs_0_), channel_id=1, source_target_pairs={{0,1},{1,0},{2,3},{3,2},{4,5},{5,4},{6,7},{7,6},{8,9},{9,8},{10,11... | collective-permute-start | bytes 786440 | tf_op jit(solution)/shard_map/ppermute | solution.py:393
  127.6 40.0 %collective-permute-start.9 = (bf16[512,256]{1,0:T(8,128)(2,1)}, bf16[512,256]{1,0:T(8,128)(2,1)}, u32[]{:S(2)}, u32[]{:S(2)}) collective-permute-start(bf16[512,256]{1,0:T(8,128)(2,1)} %collective-permute-done.8.refs_2_), channel_id=1, source_target_pairs={{0,1},{1,0},{2,3},{3,2},{4,5},{5,4},{6,7},{7,6},{8,9},{9,8},{10,11... | collective-permute-start | bytes 786440 | tf_op jit(solution)/shard_map/ppermute | solution.py:393
  (66 other events, 436.6 us)
